TPU v7x, 512 devices: a 8x2x16 block of a 8x8x16 slice. The times are simulated.
512 devices in a mesh: groups: 2 (over y), dp: 128 (over z, x), tensor: 2 (over core).
Axes of the slice: x: 8, y: 2, z: 16, core: 2. Of those that a mesh axis runs over, the one named last changes fastest.
The devices are a block of a 8x8x16 slice.
Arguments:
- cache_keys: bfloat16 [256, 2048, 1024], P(('groups', 'dp'), None, 'tensor'), parts along dimension 0, may hold values from -32 to 32
- cache_values: bfloat16 [256, 2048, 1024], P(('groups', 'dp'), None, 'tensor'), parts along dimension 0, may hold values from -6 to 6
- lengths: int32 [256], P(('groups', 'dp')), parts along dimension 0, may hold values from 512 to 2048
- parent_scores: float32 [256], P(('groups', 'dp')), parts along dimension 0, may hold values from -6 to 0
- parents: int32 [256], P(('groups', 'dp')), parts along dimension 0, may hold values from 0 to 127, as said below
- queries: bfloat16 [256, 4, 8192], P(('groups', 'dp'), None, 'tensor'), parts along dimension 0, may hold values from -32 to 32
- new_keys: bfloat16 [256, 4, 1024], P(('groups', 'dp'), None, 'tensor'), parts along dimension 0, may hold values from -9 to 9
- new_values: bfloat16 [256, 4, 1024], P(('groups', 'dp'), None, 'tensor'), parts along dimension 0, may hold values from -6 to 6
- reward_weight: bfloat16 [8192], P('tensor'), may hold values from -3 to 3
Outputs:
- attended: bfloat16 [256, 4, 8192], P(('groups', 'dp'), None, 'tensor'), parts along dimension 0
- scores: float32 [256], P(('groups', 'dp')), parts along dimension 0
There are 2 independent parts, one for each index of `groups`. A program takes and returns all parts, laid end to end along the dimension named above; an argument that names none is the same for every part. Nothing has to cross between parts.
Inputs may be any that keep to these rules, and one draw needn't show every extreme that they name: `parents`: each old beam is continued by at most 2 new slots; in every draw some old beams are continued by exactly 2 and others by none.
All inputs are finite; a program needn't handle non-finite values.
Results may differ from a plain program's by a relative error of at most 0.0056.
Values may be sent and summed in bfloat16 or wider, within the bound.
No kernel may reach another device: no remote copies, remote signals or barrier semaphores. Data moves between devices by JAX's collectives and lax.ppermute only.
A program may use at most 64 MiB of HBM per device.

v0:
```python
import math

import jax
import jax.numpy as jnp
from jax import lax
from jax.sharding import Mesh
from jax.sharding import PartitionSpec as P

HD = 128
CHILDREN = 2
DP = ("dp_0", "dp_1")
GROUPS_DP = ("groups", "dp_0", "dp_1")


def joined_along(tiles, dim):
    lengths = list(tiles.shape[1:])
    lengths[dim] *= tiles.shape[0]
    return jnp.moveaxis(tiles, 0, dim).reshape(lengths)


def stacked_from(x, axes, sequence):
    tiles = x[None]
    for k in sequence:
        tiles = lax.all_gather(tiles, axes[k], axis=0, tiled=True)
    current = [lax.axis_size(axes[k]) for k in reversed(sequence)]
    tiles = tiles.reshape(*current, *x.shape)
    turned = sorted(range(len(sequence)), key=lambda place: sequence[len(sequence) - 1 - place])
    return tiles.transpose(*turned, *range(len(sequence), tiles.ndim)).reshape(-1, *x.shape)


def gather_axes(x, axes, sequence, dim):
    return joined_along(stacked_from(x, axes, sequence), dim)


def in_one_piece(arrays, axis, dim, along):
    widths = [math.prod(a.shape[along:]) for a in arrays]
    both = jnp.concatenate(
        [a.reshape(*a.shape[:along], w) for a, w in zip(arrays, widths)], axis=along
    )
    result = lax.all_gather(both, axis, axis=dim, tiled=True)
    tiles = jnp.split(result, [sum(widths[:k]) for k in range(1, len(widths))], axis=along)
    return tuple(
        (b.reshape(*result.shape[:along], *a.shape[along:]) for a, b in zip(arrays, tiles))
    )


def over_pieces(x, axis):
    return lax.all_gather(x, axis).sum(0)


def per_device(
    cache_keys,
    cache_values,
    lengths,
    parent_scores,
    parents,
    queries,
    new_keys,
    new_values,
    reward_weight,
):
    myself = lax.axis_index(DP)
    steps = queries.shape[1]
    width = queries.shape[2]
    heads = width // HD
    kv_heads = cache_keys.shape[2] // HD
    group = heads // kv_heads
    context = cache_keys.shape[1]
    scale = HD ** (-0.5)
    everyone = gather_axes(parents, DP, (0, 1), 0)
    slot_ids = jnp.arange(everyone.shape[0])
    earlier = slot_ids[None, :] < slot_ids[:, None]
    same = everyone[None, :] == everyone[:, None]
    rank = jnp.sum((earlier & same).astype(jnp.int32), axis=1)
    mine = everyone == myself
    picker = ((jnp.arange(CHILDREN)[:, None] == rank[None, :]) & mine[None, :]).astype(jnp.bfloat16)
    valid = jnp.arange(context) < lengths[0]
    holder = lax.dynamic_index_in_dim(everyone, myself, 0, keepdims=False)
    own_rank = lax.dynamic_index_in_dim(rank, myself, 0, keepdims=False)
    wanted = holder * CHILDREN + own_rank
    gathered = jnp.dot(
        picker,
        gather_axes(queries.reshape(1, steps * width), DP, (0, 1), 0),
        preferred_element_type=jnp.float32,
    )
    rows = gathered.astype(jnp.bfloat16).reshape(CHILDREN, steps, width)
    count = rows.shape[0]
    items = rows.shape[1]
    flat = rows.reshape(count * items, kv_heads, group, HD)
    outputs = []
    log_totals = []
    for head in range(kv_heads):
        keys = cache_keys[0, :, head * HD : (head + 1) * HD]
        values = cache_values[0, :, head * HD : (head + 1) * HD]
        logits = (
            jnp.einsum("rjd,cd->rjc", flat[:, head], keys, preferred_element_type=jnp.float32)
            * scale
        )
        logits = jnp.where(valid[None, None, :], logits, -1e30)
        top_here = jnp.max(logits, axis=-1)
        weights = jnp.exp(logits - top_here[..., None])
        total = jnp.sum(weights, axis=-1)
        summed = jnp.einsum(
            "rjc,cd->rjd", weights.astype(jnp.bfloat16), values, preferred_element_type=jnp.float32
        )
        outputs.append(summed / total[..., None])
        log_totals.append(top_here + jnp.log(total))
    parent_out = jnp.stack(outputs, axis=1).reshape(count, items, width).astype(jnp.bfloat16)
    parent_lse = jnp.stack(log_totals, axis=1).reshape(count, items, heads)
    parent_out, parent_lse = (parent_out, parent_lse)
    piece = lax.all_gather(parent_out.reshape(CHILDREN, steps * width), DP, axis=0, tiled=True)
    hit = (jnp.arange(piece.shape[0]) == wanted).astype(jnp.bfloat16)
    received = jnp.dot(hit[None], piece, preferred_element_type=jnp.float32)
    carried = jnp.broadcast_to(parent_scores[0], (CHILDREN,))
    lse_all, carried_all = in_one_piece(
        (parent_lse.reshape(CHILDREN, steps * heads), carried), DP, 0, 1
    )
    sum_parent = received.reshape(steps, kv_heads, group, HD)
    top_parent = lax.dynamic_index_in_dim(lse_all, wanted, 0, keepdims=False).reshape(
        steps, kv_heads, group
    )
    inherited = lax.dynamic_index_in_dim(carried_all, wanted, 0, keepdims=False)
    query = queries[0].reshape(steps, kv_heads, group, HD)
    own_keys = new_keys[0].reshape(steps, kv_heads, HD)
    own_values = new_values[0].reshape(steps, kv_heads, HD)
    own_logits = (
        jnp.einsum("tgjd,ugd->tgju", query, own_keys, preferred_element_type=jnp.float32) * scale
    )
    causal = jnp.arange(steps)[None, :] <= jnp.arange(steps)[:, None]
    own_logits = jnp.where(causal[:, None, None, :], own_logits, -1e30)
    top_own = jnp.max(own_logits, axis=-1)
    own_weights = jnp.exp(own_logits - top_own[..., None])
    total_own = jnp.sum(own_weights, axis=-1)
    sum_own = jnp.einsum(
        "tgju,ugd->tgjd",
        own_weights.astype(jnp.bfloat16),
        own_values,
        preferred_element_type=jnp.float32,
    )
    top = jnp.maximum(top_parent, top_own)
    factor_parent = jnp.exp(top_parent - top)
    factor_own = jnp.exp(top_own - top)
    merged = (sum_parent * factor_parent[..., None] + sum_own * factor_own[..., None]) / (
        factor_parent + total_own * factor_own
    )[..., None]
    output = merged.reshape(steps, width).astype(jnp.bfloat16)
    partial_reward = jnp.dot(output, reward_weight, preferred_element_type=jnp.float32)
    reward = over_pieces(partial_reward, "tensor")
    score = inherited + jnp.sum(jax.nn.log_sigmoid(reward))
    return (output[None], score.reshape(1))


def solution(mesh):
    finer = Mesh(
        mesh.devices.reshape(mesh.shape["groups"], 16, 8, mesh.shape["tensor"]),
        ("groups", "dp_0", "dp_1", "tensor"),
    )
    return jax.shard_map(
        per_device,
        mesh=finer,
        in_specs=(
            P(GROUPS_DP, None, "tensor"),
            P(GROUPS_DP, None, "tensor"),
            P(GROUPS_DP),
            P(GROUPS_DP),
            P(GROUPS_DP),
            P(GROUPS_DP, None, "tensor"),
            P(GROUPS_DP, None, "tensor"),
            P(GROUPS_DP, None, "tensor"),
            P("tensor"),
        ),
        out_specs=(P(GROUPS_DP, None, "tensor"), P(GROUPS_DP)),
        check_vma=False,
    )
```

profile of v0, /device:TPU:65, one launch (start us, length us, event | category | flops | bytes accessed | tf_op | source)
XLA Modules:
  0.0 346.4 jit_solution(11860320179349468749)
XLA Ops:
  7.3 0.8 broadcast_in_dim_reshape.3
  8.1 68.0 %all_gather.26 = bf16[16,1,16384]{2,1,0:T(2,128)(2,1)S(1)} all-gather(bf16[1,1,16384]{2,1,0:T(2,128)(2,1)S(1)} %broadcast_in_dim_reshape.3), channel_id=1, replica_groups=mesh['groups'=2,'dp_0'=16,'dp_1'=8,'tensor'=2] {'dp_0'}, dimensions={0}, use_global_device_ids=true | all-gather | bytes 557056 | tf_op jit(solution)/shard_map/all_gather | solution.py:24
  76.1 1.4 copy.57
  78.3 1.3 dynamic-slice.1
  79.5 1.3 dynamic-slice.2
  81.5 0.8 dynamic-update-slice
  82.2 13.9 %all-reduce.1 = s32[16]{0:T(128)S(1)} all-reduce(s32[16]{0:T(128)S(1)} %dynamic-update-slice), channel_id=2, replica_groups=mesh['groups'=2,'dp_0'=16,'dp_1'=8,'tensor'=2] {'dp_0'}, use_global_device_ids=true, to_apply=%add.1 | all-reduce | flops 16 | bytes 128
  96.3 13.0 %all-reduce.2 = s32[128]{0:T(128)S(1)} all-reduce(s32[128]{0:T(128)S(1)} %dynamic-update-slice.1), channel_id=3, replica_groups=mesh['groups'=2,'dp_0'=16,'dp_1'=8,'tensor'=2] {'dp_1'}, use_global_device_ids=true, to_apply=%add.2 | all-reduce | flops 128 | bytes 1024
  110.4 28.8 %all-gather.8.cloned.1.call-done = bf16[128,1,16384]{2,0,1:T(8,128)(2,1)} async-done(((bf16[16,1,16384]{2,0,1:T(8,128)(2,1)}), bf16[128,1,16384]{2,0,1:T(8,128)(2,1)}) %all-gather.8.cloned.1.call-update) | async-done | bytes 4194320 | tf_op jit(solution)/shard_map/all_gather | solution.py:24
  139.2 4.7 %convolution_convert_fusion = bf16[2,16384]{1,0:T(2,128)(2,1)S(1)} fusion(bf16[16,8,1,16384]{3,0,1,2:T(8,128)(2,1)} %bitcast.171, pred[128]{0:T(512)(128)(4,1)S(1)} %broadcast_compare_fusion, s32[128]{0:T(128)S(1)} %convert_reduce_fusion), kind=kOutput, calls=%fused_computation | convolution fusion | flops 8421888 | bytes 4260480 | tf_op jit(solution)/shard_map/dot_general | solution.py:81
  143.9 0.4 fusion.73
  144.3 0.4 fusion.74
  144.7 0.4 fusion.75
  145.1 0.4 fusion.76
  145.9 0.3 fusion.18
  146.4 0.3 fusion.19
  147.0 0.3 fusion.20
  147.5 0.3 fusion.21
  147.8 0.7 reshape.190
  148.5 0.6 dynamic_slice.15
  149.1 0.6 dynamic_slice.16
  151.7 1.2 dynamic-slice.3
  153.5 0.3 fusion.77
  154.0 80.8 %all-gather.4 = f32[128,2,129]{2,1,0:T(2,128)S(1)} all-gather(f32[1,2,129]{2,1,0:T(2,128)S(1)} %pad_bitcast_fusion), channel_id=1, replica_groups=mesh['groups'=2,'dp_0'=16,'dp_1'=8,'tensor'=2] {'dp_0','dp_1'}, dimensions={0}, use_global_device_ids=true | all-gather | bytes 133128 | tf_op jit(solution)/shard_map/all_gather | solution.py:40
  235.1 0.5 constant_dynamic-slice_fusion
  235.7 58.1 %all-gather.10.cloned.1.call-done = bf16[128,2,16384]{2,1,0:T(2,128)(2,1)} async-done(((bf16[1,2,16384]{2,1,0:T(2,128)(2,1)}), bf16[128,2,16384]{2,1,0:T(2,128)(2,1)}) %all-gather.10.cloned.1.call-update) | async-done | bytes 8388624 | tf_op jit(solution)/shard_map/all_gather | solution.py:111
  293.8 13.1 %reshape.191 = bf16[256,16384]{1,0:T(8,128)(2,1)} reshape(bf16[128,2,16384]{2,1,0:T(2,128)(2,1)} %all-gather.10.cloned.1.call-done) | data formatting | bytes 16777216
  306.9 9.2 %copy.81 = bf16[32,8,128,128]{3,2,1,0:T(8,128)(2,1)} copy(bf16[32,8,128,128]{3,1,2,0:T(8,128)(2,1)} %bitcast.170) | data formatting | bytes 16777216
  316.1 7.9 %fusion = f32[1,4,4,8,128]{4,0,3,2,1:T(1,128)S(1)} fusion(bf16[4,4,8,128,256]{3,2,1,0,4:T(8,128)(2,1)} %bitcast.169, pred[256,1,1,1,1]{0,1,2,3,4:T(4,128)(4,1)S(1)} %reshape.209), kind=kOutput, calls=%fused_computation.1 | convolution fusion | flops 8388608 | bytes 8454400 | tf_op jit(solution)/shard_map/dot_general | solution.py:113
  324.5 0.6 convert_element_type.53
  325.1 11.1 %all-reduce.3 = f32[8]{0:T(128)S(1)} all-reduce(f32[8]{0:T(128)S(1)} %dynamic-update-slice.2), channel_id=4, replica_groups=mesh['groups'=2,'dp_0'=16,'dp_1'=8,'tensor'=2] {'tensor'}, use_global_device_ids=true, to_apply=%add.3 | all-reduce | flops 8 | bytes 64
  336.4 0.7 fusion.69
  (56 shorter events, 3.3 us)
Async XLA Ops:
  7.2 316.7 %copy-start = (bf16[1,4,512]{2,1,0:T(4,128)(2,1)S(1)}, bf16[1,4,512]{2,1,0:T(4,128)(2,1)}, u32[]{:S(2)}) copy-start(bf16[1,4,512]{2,1,0:T(4,128)(2,1)} %param.16) | copy-start | bytes 12292
  7.2 132.0 %all-gather.8.cloned.1.call-start = ((), (), s32[]{:S(2)}) async-start(), calls=%async_computation | async-start | bytes 4718592 | tf_op jit(solution)/shard_map/all_gather | solution.py:24
  77.5 216.2 %all-gather.10.cloned.1.call-start = ((), (), s32[]{:S(2)}) async-start(), calls=%async_computation.1 | async-start | bytes 8454144 | tf_op jit(solution)/shard_map/all_gather | solution.py:111
  139.2 4.7 %copy-start.1 = (bf16[1,2048,512]{2,1,0:T(8,128)(2,1)S(1)}, bf16[1,2048,512]{2,1,0:T(8,128)(2,1)}, u32[]{:S(2)}) copy-start(bf16[1,2048,512]{2,1,0:T(8,128)(2,1)} %param.9) | copy-start | bytes 6291460
  144.3 1.6 copy-start.2
  146.7 5.0 %copy-start.4 = (bf16[4096]{0:T(1024)(128)(2,1)S(1)}, bf16[4096]{0:T(1024)(128)(2,1)}, u32[]{:S(2)}) copy-start(bf16[4096]{0:T(1024)(128)(2,1)} %param.17) | copy-start | bytes 24580
  146.7 6.8 %copy-start.3 = (bf16[1,4,4096]{2,1,0:T(4,128)(2,1)S(1)}, bf16[1,4,4096]{2,1,0:T(4,128)(2,1)}, u32[]{:S(2)}) copy-start(bf16[1,4,4096]{2,1,0:T(4,128)(2,1)} %param.14) | copy-start | bytes 98308
  146.7 6.8 %copy-start.5 = (bf16[1,4,512]{2,1,0:T(4,128)(2,1)S(1)}, bf16[1,4,512]{2,1,0:T(4,128)(2,1)}, u32[]{:S(2)}) copy-start(bf16[1,4,512]{2,1,0:T(4,128)(2,1)} %param.15) | copy-start | bytes 12292
Sparse Core Ops, SparseCore 0:
  77.7 61.4 all-gather.7
  148.7 145.0 all-gather.9
where the time goes:
time: 347 us; the launch traced here: 346 us
  blocking collectives  187 us (54%)
  waiting for transfers between devices  87 us (25%)
  local copies, waits for them, and re-layouts  33.5 us (10%)
  between operations  21.3 us (6%)
  matrix products  15.8 us (5%)
    all_gather x1, blocking collectives, in_one_piece(): result = lax.all_gather(both, axis, axis=dim, tiled=True)  80.8 us
    all_gather x1, blocking collectives, stacked_from(): tiles = lax.all_gather(tiles, axes[k], axis=0, tiled=True)  68 us
    all_gather x1, waiting for transfers between devices, per_device(): lax.all_gather(parent_out.reshape(CHILDREN, steps * width), DP, axis=0, t...  58.1 us
    unnamed x3, blocking collectives  38 us
    all_gather x1, waiting for transfers between devices, stacked_from(): tiles = lax.all_gather(tiles, axes[k], axis=0, tiled=True)  28.8 us
    unnamed x27, local copies, waits for them, and re-layouts  28.3 us
    dot_general x1, matrix products, per_device(): received = jnp.dot(hit[None], piece, preferred_element_type=jnp.float32)  7.85 us
  transfers between devices with their start and end apart: 2, of which 2 were waited for; matrix products, arithmetic and copies ran while one was open for 2% of the time, Pallas kernels for 0%

commit v1 on v0

v1 whole, which is shorter than its diff:
```python
import functools

import jax
import jax.numpy as jnp
from jax import lax
from jax.experimental import pallas as pl
from jax.experimental.pallas import tpu as pltpu
from jax.sharding import Mesh
from jax.sharding import PartitionSpec as P

HD = 128
CHILDREN = 2
META = 8
GROUPS_DP = ("groups", "z", "x")
VMEM = pl.BlockSpec(memory_space=pltpu.VMEM)
SMEM = pl.BlockSpec(memory_space=pltpu.SMEM)
BF16 = jnp.bfloat16
F32 = jnp.float32


def number_in(ref, i, row):
    return jnp.max(ref[i, row : row + META, :].astype(F32)[0:1, :]).astype(jnp.int32)


def filled(value):
    return jnp.full((META, HD), value, F32).astype(BF16)


def as_row(column):
    n = column.shape[0]
    rows = lax.broadcasted_iota(jnp.int32, (n, HD), 0)
    lanes = lax.broadcasted_iota(jnp.int32, (n, HD), 1)
    return jnp.sum(jnp.where(rows == lanes, column, 0.0), axis=0, keepdims=True)


def as_column(row):
    n = row.shape[1]
    rows = lax.broadcasted_iota(jnp.int32, (n, n), 0)
    lanes = lax.broadcasted_iota(jnp.int32, (n, n), 1)
    return jnp.sum(jnp.where(rows == lanes, row, 0.0), axis=1, keepdims=True)


def in_parts(x):
    first = x.astype(BF16)
    rest = x - first.astype(F32)
    second = rest.astype(BF16)
    third = (rest - second.astype(F32)).astype(BF16)
    return first, second, third


def items_of(q_ref, steps, heads):
    return [q_ref[0, :, h * HD : (h + 1) * HD] for h in range(heads)]


def send_kernel(parents_ref, q_ref, out_ref, item):
    steps, heads = q_ref.shape[1], q_ref.shape[2] // HD
    size = steps * heads
    for h in range(heads):
        item[h * steps : (h + 1) * steps, :] = q_ref[0, :, h * HD : (h + 1) * HD].astype(F32)
    item[size : size + META, :] = jnp.full((META, HD), parents_ref[0].astype(F32), F32)
    packed = item[...].astype(BF16)
    for d in range(out_ref.shape[0]):
        out_ref[d] = packed


def turn_kernel(columns, in_ref, out_ref, used):
    size = in_ref.shape[1] - META
    my_row, my_column = lax.axis_index("z"), lax.axis_index("x")
    for i in range(out_ref.shape[0]):
        out_ref[i, size:, :] = filled(-1.0)
    for i in range(columns):
        used[i] = 0
    for i in range(in_ref.shape[0]):
        parent = number_in(in_ref, i, size)
        row, column = parent // columns, parent % columns

        @pl.when(row == my_row)
        def _():
            place = used[column]
            used[column] = place + 1
            out_ref[column * CHILDREN + place, :size, :] = in_ref[i, :size, :]
            out_ref[column * CHILDREN + place, size:, :] = filled((i * columns + my_column).astype(F32))


def attend_kernel(kv_heads, lengths_ref, scores_ref, in_ref, k_ref, v_ref, out_ref, q, item, found):
    size = in_ref.shape[1] - META
    context = k_ref.shape[1]
    rows = size // kv_heads
    q[...] = jnp.zeros_like(q)
    found[0] = 0
    for c in range(CHILDREN):
        found[1 + c] = -1
    for i in range(in_ref.shape[0]):
        child = number_in(in_ref, i, size)

        @pl.when(child >= 0)
        def _():
            n = found[0]
            found[0] = n + 1
            found[1 + n] = child
            q[n] = in_ref[i, :size, :]

    scale = HD**-0.5
    valid = lax.broadcasted_iota(jnp.int32, (CHILDREN * rows, context), 1) < lengths_ref[0]
    totals = [[] for _ in range(CHILDREN)]
    for k in range(kv_heads):
        keys = k_ref[0, :, k * HD : (k + 1) * HD]
        values = v_ref[0, :, k * HD : (k + 1) * HD]
        both = jnp.concatenate([q[c, k * rows : (k + 1) * rows, :] for c in range(CHILDREN)], axis=0)
        logits = (
            lax.dot_general(both, keys, (((1,), (1,)), ((), ())), preferred_element_type=F32)
            * scale
        )
        logits = jnp.where(valid, logits, -1e30)
        top = jnp.max(logits, axis=-1, keepdims=True)
        weights = jnp.exp(logits - top)
        total = jnp.sum(weights, axis=-1, keepdims=True)
        summed = jnp.dot(weights.astype(BF16), values, preferred_element_type=F32)
        result = (summed / total).astype(BF16)
        log_total = top + jnp.log(total)
        for c in range(CHILDREN):
            item[c, k * rows : (k + 1) * rows, :] = result[c * rows : (c + 1) * rows, :]
            totals[c].append(log_total[c * rows : (c + 1) * rows, :])
    score = in_parts(jnp.full((1, HD), scores_ref[0], F32))
    for c in range(CHILDREN):
        line = in_parts(as_row(jnp.concatenate(totals[c], axis=0)))
        child = jnp.full((1, HD), found[1 + c].astype(F32), F32)
        tail = [child, *line, *score, jnp.zeros((1, HD), F32)]
        item[c, size:, :] = jnp.concatenate([t.astype(F32) for t in tail], axis=0).astype(BF16)
    for d in range(out_ref.shape[0] // CHILDREN):
        for c in range(CHILDREN):
            out_ref[d * CHILDREN + c] = item[c]


def back_kernel(columns, in_ref, out_ref):
    size = in_ref.shape[1] - META
    my_column = lax.axis_index("x")
    for i in range(in_ref.shape[0]):
        child = number_in(in_ref, i, size)

        @pl.when((child >= 0) & (child % columns == my_column))
        def _():
            out_ref[child // columns] = in_ref[i]


def merge_kernel(columns, parents_ref, in_ref, q_ref, nk_ref, nv_ref, rw_ref, out_ref, reward_ref, spare_ref, wide):
    size = in_ref.shape[1] - META
    steps, heads = q_ref.shape[1], q_ref.shape[2] // HD
    kv_heads = nk_ref.shape[2] // HD
    rows = size // kv_heads
    slot = parents_ref[0] // columns
    sum_parent = in_ref[slot, :size, :].astype(F32)
    tail = in_ref[slot, size:, :].astype(F32)
    top_parent = as_column((tail[1:2] + tail[2:3]) + tail[3:4])
    spare_ref[...] = jnp.broadcast_to((tail[4:5] + tail[5:6]) + tail[6:7], spare_ref.shape)
    for h in range(heads):
        wide[h * steps : (h + 1) * steps, :] = q_ref[0, :, h * HD : (h + 1) * HD].astype(F32)
    query = wide[...]
    step = lax.broadcasted_iota(jnp.int32, (size, 1), 0) % steps

    def spread(ref, u):
        return jnp.concatenate(
            [
                jnp.broadcast_to(ref[0, u : u + 1, k * HD : (k + 1) * HD].astype(F32), (rows, HD))
                for k in range(kv_heads)
            ],
            axis=0,
        )

    scale = HD**-0.5
    logits = [
        jnp.where(u <= step, jnp.sum(query * spread(nk_ref, u), axis=-1, keepdims=True) * scale, -1e30)
        for u in range(steps)
    ]
    top_own = functools.reduce(jnp.maximum, logits)
    weights = [jnp.exp(x - top_own) for x in logits]
    total_own = functools.reduce(jnp.add, weights)
    sum_own = functools.reduce(
        jnp.add, [w.astype(BF16).astype(F32) * spread(nv_ref, u) for u, w in enumerate(weights)]
    )
    top = jnp.maximum(top_parent, top_own)
    factor_parent = jnp.exp(top_parent - top)
    factor_own = jnp.exp(top_own - top)
    merged = (sum_parent * factor_parent + sum_own * factor_own) / (
        factor_parent + total_own * factor_own
    )
    attended = merged.astype(BF16).astype(F32)
    wide[...] = attended
    reward = jnp.zeros((steps, HD), F32)
    for h in range(heads):
        part = wide[h * steps : (h + 1) * steps, :]
        out_ref[0, :, h * HD : (h + 1) * HD] = part.astype(BF16)
        reward = reward + part * rw_ref[0:1, h * HD : (h + 1) * HD].astype(F32)
    reward_ref[...] = jnp.broadcast_to(jnp.sum(reward, axis=-1, keepdims=True), reward_ref.shape)


def per_device(
    cache_keys,
    cache_values,
    lengths,
    parent_scores,
    parents,
    queries,
    new_keys,
    new_values,
    reward_weight,
):
    z, x = lax.axis_size("z"), lax.axis_size("x")
    steps, width = queries.shape[1:]
    heads = width // HD
    kv_heads = cache_keys.shape[2] // HD
    size = steps * heads
    tall = size + META

    def items(n):
        return jax.ShapeDtypeStruct((n, tall, HD), BF16)

    sent = pl.pallas_call(
        send_kernel,
        out_shape=items(z),
        in_specs=[SMEM, VMEM],
        out_specs=VMEM,
        scratch_shapes=[pltpu.VMEM((tall, HD), F32)],
        name="send",
    )(parents, queries)
    column = lax.all_to_all(sent, "z", 0, 0, tiled=True)
    turned = pl.pallas_call(
        functools.partial(turn_kernel, x),
        out_shape=items(x * CHILDREN),
        in_specs=[VMEM],
        out_specs=VMEM,
        scratch_shapes=[pltpu.SMEM((x,), jnp.int32)],
        name="turn",
    )(column)
    row = lax.all_to_all(turned, "x", 0, 0, tiled=True)
    outputs = pl.pallas_call(
        functools.partial(attend_kernel, kv_heads),
        out_shape=items(x * CHILDREN),
        in_specs=[SMEM, SMEM, VMEM, VMEM, VMEM],
        out_specs=VMEM,
        scratch_shapes=[
            pltpu.VMEM((CHILDREN, size, HD), BF16),
            pltpu.VMEM((CHILDREN, tall, HD), BF16),
            pltpu.SMEM((1 + CHILDREN,), jnp.int32),
        ],
        name="attend",
    )(lengths, parent_scores, row, cache_keys, cache_values)
    row = lax.all_to_all(outputs, "x", 0, 0, tiled=True)
    back = pl.pallas_call(
        functools.partial(back_kernel, x),
        out_shape=items(z),
        in_specs=[VMEM],
        out_specs=VMEM,
        name="back",
    )(row)
    column = lax.all_to_all(back, "z", 0, 0, tiled=True)
    output, partial_reward, inherited = pl.pallas_call(
        functools.partial(merge_kernel, x),
        out_shape=(
            jax.ShapeDtypeStruct(queries.shape, BF16),
            jax.ShapeDtypeStruct((steps, HD), F32),
            jax.ShapeDtypeStruct((1, HD), F32),
        ),
        in_specs=[SMEM, VMEM, VMEM, VMEM, VMEM, VMEM],
        out_specs=(VMEM, VMEM, VMEM),
        scratch_shapes=[pltpu.VMEM((size, HD), F32)],
        name="merge",
    )(parents, column, queries, new_keys, new_values, reward_weight.reshape(1, width))
    reward = lax.psum(partial_reward, "tensor")[:, 0]
    score = inherited[0, :1] + jnp.sum(jax.nn.log_sigmoid(reward))
    return (output, score)


def solution(mesh):
    finer = Mesh(
        mesh.devices.reshape(mesh.shape["groups"], 16, 8, mesh.shape["tensor"]),
        ("groups", "z", "x", "tensor"),
    )
    return jax.shard_map(
        per_device,
        mesh=finer,
        in_specs=(
            P(GROUPS_DP, None, "tensor"),
            P(GROUPS_DP, None, "tensor"),
            P(GROUPS_DP),
            P(GROUPS_DP),
            P(GROUPS_DP),
            P(GROUPS_DP, None, "tensor"),
            P(GROUPS_DP, None, "tensor"),
            P(GROUPS_DP, None, "tensor"),
            P("tensor"),
        ),
        out_specs=(P(GROUPS_DP, None, "tensor"), P(GROUPS_DP)),
        check_vma=False,
    )
```

time: 347 us -> 188 us (0.54)
  blocking collectives: 187 us -> 103 us
  waiting for transfers between devices: 87 us -> 37.5 us
  local copies, waits for them, and re-layouts: 33.5 us -> 2.21 us
  starting transfers between devices: 0.13 us -> 19.6 us
  Pallas kernels: 0 us -> 18.8 us
  between operations: 21.3 us -> 5.07 us
  matrix products: 15.8 us -> 0 us
    all_gather x2 -> x0, blocking collectives: 149 us -> none  [the longest x1 80.8 us: in_one_piece(): result = lax.all_gather(both, axis, axis=dim, tiled=True)]
    all_to_all x0 -> x2, blocking collectives: none -> 94.2 us  [the longest x1 76.4 us: per_device(): column = lax.all_to_all(sent, 'z', 0, 0, tiled=True)]
    all_gather x2 -> x0, waiting for transfers between devices: 86.9 us -> none  [the longest x1 58.1 us: per_device(): lax.all_gather(parent_out.reshape(CHILDREN, steps * width), DP, axis=0, t...]
    unnamed x3 -> x0, blocking collectives: 38 us -> none
    all_to_all x0 -> x2, waiting for transfers between devices: none -> 37.5 us  [the longest x1 23.5 us: per_device(): column = lax.all_to_all(back, 'z', 0, 0, tiled=True)]
    unnamed x27 -> x6, local copies, waits for them, and re-layouts: 28.3 us -> 1.59 us
    all_to_all x0 -> x2, starting transfers between devices: none -> 19.6 us  [the longest x1 12.5 us: per_device(): column = lax.all_to_all(back, 'z', 0, 0, tiled=True)]
    pallas_call x0 -> x5, Pallas kernels: none -> 18.8 us  [the longest x1 7.33 us: per_device(): pl.pallas_call(functools.partial(attend_kernel, kv_heads), out_shape=item...]
  transfers between devices with their start and end apart: 2 -> 2, of which waited for: 2 -> 2; matrix products, arithmetic and copies ran while one was open for 2% -> 0% of each run, Pallas kernels for 0% -> 0%
where the time goes in v1:
time: 188 us; the launch traced here: 187 us
  blocking collectives  103 us (55%)
  waiting for transfers between devices  37.5 us (20%)
  starting transfers between devices  19.6 us (10%)
  Pallas kernels  18.8 us (10%)
  between operations  5.07 us (3%)
  local copies, waits for them, and re-layouts  2.21 us (1%)
    all_to_all x1, blocking collectives, per_device(): column = lax.all_to_all(sent, 'z', 0, 0, tiled=True)  76.4 us
    all_to_all x1, waiting for transfers between devices, per_device(): column = lax.all_to_all(back, 'z', 0, 0, tiled=True)  23.5 us
    all_to_all x1, blocking collectives, per_device(): row = lax.all_to_all(outputs, 'x', 0, 0, tiled=True)  17.8 us
    all_to_all x1, waiting for transfers between devices, per_device(): row = lax.all_to_all(turned, 'x', 0, 0, tiled=True)  14 us
    all_to_all x1, starting transfers between devices, per_device(): column = lax.all_to_all(back, 'z', 0, 0, tiled=True)  12.5 us
    psum x1, blocking collectives, per_device(): reward = lax.psum(partial_reward, 'tensor')[:, 0]  8.74 us
    pallas_call x1, Pallas kernels, per_device(): pl.pallas_call(functools.partial(attend_kernel, kv_heads), out_shape=item...  7.33 us
    all_to_all x1, starting transfers between devices, per_device(): row = lax.all_to_all(turned, 'x', 0, 0, tiled=True)  7.06 us
  transfers between devices with their start and end apart: 2, of which 2 were waited for; matrix products, arithmetic and copies ran while one was open for 0% of the time, Pallas kernels for 0%

profile of v1, /device:TPU:65, one launch (start us, length us, event | category | flops | bytes accessed | tf_op | source)
XLA Modules:
  0.0 186.9 jit_solution(976534882380869956)
XLA Ops:
  1.3 1.6 send.1
  2.9 76.4 %all_to_all.20.in_ref = bf16[16,136,128]{2,1,0:T(8,128)(2,1)} all-to-all(bf16[16,136,128]{2,1,0:T(8,128)(2,1)} %send.1), channel_id=1, replica_groups=mesh['groups'=2,'z'=16,'x'=8,'tensor'=2] {'z'}, dimensions={0} | all-to-all | bytes 1114112 | tf_op jit(solution)/shard_map/all_to_all | solution.py:226
  79.3 3.9 %turn.1 = bf16[16,136,128]{2,1,0:T(8,128)(2,1)} custom-call(bf16[16,136,128]{2,1,0:T(8,128)(2,1)} %all_to_all.20.in_ref), custom_call_target="tpu_custom_call" | custom-call | tf_op jit(solution)/shard_map/turn/pallas_call | solution.py:227
  83.2 7.1 %all-to-all-start.1 = ((bf16[16,136,128]{2,1,0:T(8,128)(2,1)}), bf16[16,136,128]{2,1,0:T(8,128)(2,1)S(1)}, u32[]{:S(2)}, u32[]{:S(2)}) async-start(bf16[16,136,128]{2,1,0:T(8,128)(2,1)} %turn.1), calls=%async_computation.1 | async-start | bytes 1114112 | tf_op jit(solution)/shard_map/all_to_all | solution.py:235
  91.6 14.0 %all-to-all-done.1.in_ref = bf16[16,136,128]{2,1,0:T(8,128)(2,1)S(1)} async-done(((bf16[16,136,128]{2,1,0:T(8,128)(2,1)}), bf16[16,136,128]{2,1,0:T(8,128)(2,1)S(1)}, u32[]{:S(2)}, u32[]{:S(2)}) %all-to-all-start.1) | async-done | bytes 557088 | tf_op jit(solution)/shard_map/all_to_all | solution.py:235
  105.6 0.0 copy-start
  105.6 0.8 copy-done
  106.4 7.3 %attend.1 = bf16[16,136,128]{2,1,0:T(8,128)(2,1)} custom-call(s32[1]{0:T(128)S(6)} %copy.11.lengths_ref, f32[1]{0:T(128)S(6)} %copy.12.scores_ref, bf16[16,136,128]{2,1,0:T(8,128)(2,1)} %copy-done, bf16[1,2048,512]{2,1,0:T(8,128)(2,1)} %k_ref.1, bf16[1,2048,512]{2,1,0:T(8,128)(2,1)} %v_ref.1), custom_call_target="tpu_custom_call" | custom-call | tf_op jit(solution)/shard_map/attend/pallas_call | solution.py:236
  113.8 0.0 copy-start.2
  113.8 17.8 %all_to_all.21.in_ref = bf16[16,136,128]{2,1,0:T(8,128)(2,1)} all-to-all(bf16[16,136,128]{2,1,0:T(8,128)(2,1)} %attend.1), channel_id=1, replica_groups=mesh['groups'=2,'z'=16,'x'=8,'tensor'=2] {'x'}, dimensions={0} | all-to-all | bytes 1114112 | tf_op jit(solution)/shard_map/all_to_all | solution.py:248
  131.6 3.9 %back.1 = bf16[16,136,128]{2,1,0:T(8,128)(2,1)} custom-call(bf16[16,136,128]{2,1,0:T(8,128)(2,1)} %all_to_all.21.in_ref), custom_call_target="tpu_custom_call" | custom-call | tf_op jit(solution)/shard_map/back/pallas_call | solution.py:249
  135.5 12.5 %all-to-all-start.3 = ((bf16[16,136,128]{2,1,0:T(8,128)(2,1)}), bf16[16,136,128]{2,1,0:T(8,128)(2,1)S(1)}, u32[]{:S(2)}, u32[]{:S(2)}) async-start(bf16[16,136,128]{2,1,0:T(8,128)(2,1)} %back.1), calls=%async_computation.3 | async-start | bytes 1114112 | tf_op jit(solution)/shard_map/all_to_all | solution.py:256
  148.0 0.0 copy-done.2
  148.0 0.6 reshape.8.rw_ref
  148.6 23.5 %all-to-all-done.3.in_ref = bf16[16,136,128]{2,1,0:T(8,128)(2,1)S(1)} async-done(((bf16[16,136,128]{2,1,0:T(8,128)(2,1)}), bf16[16,136,128]{2,1,0:T(8,128)(2,1)S(1)}, u32[]{:S(2)}, u32[]{:S(2)}) %all-to-all-start.3) | async-done | bytes 557088 | tf_op jit(solution)/shard_map/all_to_all | solution.py:256
  172.1 0.0 copy-start.1
  172.1 0.8 copy-done.1
  172.9 2.0 %merge.1 = (bf16[1,4,4096]{2,1,0:T(4,128)(2,1)}, f32[4,128]{1,0:T(4,128)}, f32[1,128]{1,0:T(1,128)}) custom-call(s32[1]{0:T(128)S(6)} %copy.13.parents_ref, bf16[16,136,128]{2,1,0:T(8,128)(2,1)} %copy-done.1, bf16[1,4,4096]{2,1,0:T(4,128)(2,1)} %q_ref.3, bf16[1,4,512]{2,1,0:T(4,128)(2,1)} %nk_ref.1, bf16[1,4,512]{2,1,0:T(4,128)(2,1)} %nv_ref.1, ...), custom_call_target="tpu_custom_call" | custom-call | tf_op jit(solution)/shard_map/merge/pallas_call | solution.py:257
  174.9 8.7 %psum.7 = f32[4,128]{1,0:T(4,128)S(1)} all-reduce(f32[4,128]{1,0:T(4,128)} %get-tuple-element.7), channel_id=1, replica_groups=mesh['groups'=2,'z'=16,'x'=8,'tensor'=2] {'tensor'}, use_global_device_ids=true, to_apply=%region_0.0 | all-reduce | flops 512 | bytes 4096 | tf_op jit(solution)/shard_map/psum | solution.py:269
  183.7 0.1 negate_reduce_fusion
  183.8 0.7 fusion
Async XLA Ops:
  83.2 22.4 %all-to-all-start.1 = ((bf16[16,136,128]{2,1,0:T(8,128)(2,1)}), bf16[16,136,128]{2,1,0:T(8,128)(2,1)S(1)}, u32[]{:S(2)}, u32[]{:S(2)}) async-start(bf16[16,136,128]{2,1,0:T(8,128)(2,1)} %turn.1), calls=%async_computation.1 | async-start | bytes 1114112 | tf_op jit(solution)/shard_map/all_to_all | solution.py:235
  105.6 0.8 copy-start
  113.8 34.3 %copy-start.2 = (bf16[4096]{0:T(1024)(128)(2,1)S(1)}, bf16[4096]{0:T(1024)(128)(2,1)}, u32[]{:S(2)}) copy-start(bf16[4096]{0:T(1024)(128)(2,1)} %param.17) | copy-start | bytes 24580
  135.5 36.6 %all-to-all-start.3 = ((bf16[16,136,128]{2,1,0:T(8,128)(2,1)}), bf16[16,136,128]{2,1,0:T(8,128)(2,1)S(1)}, u32[]{:S(2)}, u32[]{:S(2)}) async-start(bf16[16,136,128]{2,1,0:T(8,128)(2,1)} %back.1), calls=%async_computation.3 | async-start | bytes 1114112 | tf_op jit(solution)/shard_map/all_to_all | solution.py:256
  172.1 0.8 copy-start.1

commit v2 on v1

v2 whole, which is shorter than its diff:
```python
import functools

import jax
import jax.numpy as jnp
from jax import lax
from jax.experimental import pallas as pl
from jax.experimental.pallas import tpu as pltpu
from jax.sharding import Mesh
from jax.sharding import PartitionSpec as P

HD = 128
CHILDREN = 2
META = 8
GROUPS_DP = ("groups", "zh", "zl", "x")
NEAR = ("zl", "x")
FAR = ("zh", "zl")
VMEM = pl.BlockSpec(memory_space=pltpu.VMEM)
SMEM = pl.BlockSpec(memory_space=pltpu.SMEM)
BF16 = jnp.bfloat16
F32 = jnp.float32


def limit(mib):
    return pltpu.CompilerParams(vmem_limit_bytes=mib * 1024 * 1024)


def whole_number(row, lane):
    return jnp.sum(row[:, lane : lane + 1]).astype(jnp.int32)


def in_parts(x):
    first = x.astype(BF16)
    rest = x - first.astype(F32)
    second = rest.astype(BF16)
    third = (rest - second.astype(F32)).astype(BF16)
    return [part.astype(F32) for part in (first, second, third)]


def send_kernel(columns, parents_ref, q_ref, out_ref, item):
    steps, heads = q_ref.shape[1], q_ref.shape[2] // HD
    rows = out_ref.shape[1] - META
    for h in range(heads):
        item[h * steps : (h + 1) * steps, :] = q_ref[0, :, h * HD : (h + 1) * HD].astype(F32)
    parent = jnp.full((META, HD), parents_ref[0].astype(F32), F32).astype(BF16)
    for j in range(out_ref.shape[0] // columns):
        piece = item[j * rows : (j + 1) * rows, :].astype(BF16)
        for d in range(columns):
            out_ref[j * columns + d, :rows, :] = piece
            out_ref[j * columns + d, rows:, :] = parent


def turn_kernel(columns, in_ref, out_ref, used, meta):
    rows = in_ref.shape[1] - META
    block = in_ref.shape[0] // columns
    first = lax.axis_index("zh") * block
    mine = lax.axis_index("x")
    parents = [whole_number(in_ref[i, rows:, :].astype(F32)[0:1], 0) for i in range(in_ref.shape[0])]
    meta[...] = jnp.full(meta.shape, -1.0, F32)
    for i in range(out_ref.shape[0]):
        used[i] = 0
    for i, parent in enumerate(parents):

        @pl.when(parent % columns == mine)
        def _():
            row = parent // columns
            place = used[row]
            used[row] = place + 1
            out_ref[row, pl.ds(pl.multiple_of(place * rows, rows), rows), :] = in_ref[i, :rows, :]
            child = first * columns + i
            meta[row, pl.ds(place, 1), :] = jnp.full((1, HD), child.astype(F32), F32)

    for i in range(out_ref.shape[0]):
        out_ref[i, CHILDREN * rows :, :] = meta[i].astype(BF16)


def attend_kernel(lengths_ref, scores_ref, in_ref, k_ref, v_ref, out_ref, q, item, found):
    kv_heads, tall = item.shape[:2]
    rows = (tall - META) // CHILDREN
    context = k_ref.shape[1]
    blocks = in_ref.shape[0] // kv_heads
    ids = []
    for b in range(blocks):
        tail = in_ref[b * kv_heads, CHILDREN * rows :, :].astype(F32)
        ids.append([whole_number(tail[c : c + 1], 0) for c in range(CHILDREN)])
    q[...] = jnp.zeros_like(q)
    found[0] = 0
    for c in range(CHILDREN):
        found[1 + c] = -1
    for b in range(blocks):
        for c in range(CHILDREN):

            @pl.when(ids[b][c] >= 0)
            def _():
                n = found[0]
                found[0] = n + 1
                found[1 + n] = ids[b][c]
                for j in range(kv_heads):
                    piece = in_ref[b * kv_heads + j, c * rows : (c + 1) * rows, :]
                    q[j, pl.ds(pl.multiple_of(n * rows, rows), rows), :] = piece

    scale = HD**-0.5
    valid = lax.broadcasted_iota(jnp.int32, (CHILDREN * rows, context), 1) < lengths_ref[0]
    lane = lax.broadcasted_iota(jnp.int32, (rows, HD), 1)
    diagonal = lane % rows == lax.broadcasted_iota(jnp.int32, (rows, HD), 0)
    part = lax.broadcasted_iota(jnp.int32, (1, HD), 1)
    score = in_parts(jnp.full((1, HD), scores_ref[0], F32))
    for j in range(kv_heads):
        keys = k_ref[0, :, j * HD : (j + 1) * HD]
        values = v_ref[0, :, j * HD : (j + 1) * HD]
        logits = (
            lax.dot_general(q[j], keys, (((1,), (1,)), ((), ())), preferred_element_type=F32)
            * scale
        )
        logits = jnp.where(valid, logits, -1e30)
        top = jnp.max(logits, axis=-1, keepdims=True)
        weights = jnp.exp(logits - top)
        total = jnp.sum(weights, axis=-1, keepdims=True)
        summed = jnp.dot(weights.astype(BF16), values, preferred_element_type=F32)
        item[j, : CHILDREN * rows, :] = (summed / total).astype(BF16)
        log_total = top + jnp.log(total)
        tails = []
        for c in range(CHILDREN):
            parts = in_parts(jnp.broadcast_to(log_total[c * rows : (c + 1) * rows], (rows, HD)))
            chosen = jnp.where(
                lane < rows, parts[0], jnp.where(lane < 2 * rows, parts[1], parts[2])
            )
            line = jnp.sum(jnp.where(diagonal, chosen, 0.0), axis=0, keepdims=True)
            for n, extra in enumerate([jnp.full((1, HD), found[1 + c].astype(F32), F32), *score]):
                line = jnp.where(part == 3 * rows + n, extra, line)
            tails.append(line)
        tails.append(jnp.zeros((META - CHILDREN, HD), F32))
        item[j, CHILDREN * rows :, :] = jnp.concatenate(tails, axis=0).astype(BF16)
    for b in range(blocks):
        out_ref[b * kv_heads : (b + 1) * kv_heads] = item[...]


def back_kernel(columns, in_ref, out_ref):
    rows = out_ref.shape[1] - META
    first = lax.axis_index("zh") * out_ref.shape[0]
    children = []
    for i in range(in_ref.shape[0]):
        tail = in_ref[i, CHILDREN * rows :, :].astype(F32)
        children.append([whole_number(tail[c : c + 1], 3 * rows) for c in range(CHILDREN)])
    for i in range(in_ref.shape[0]):
        for c in range(CHILDREN):
            place = children[i][c] - first

            @pl.when((place >= 0) & (place < out_ref.shape[0]))
            def _():
                out_ref[place, :rows, :] = in_ref[i, c * rows : (c + 1) * rows, :]
                tail = in_ref[i, CHILDREN * rows :, :].astype(F32)[c : c + 1]
                out_ref[place, rows:, :] = jnp.broadcast_to(tail, (META, HD)).astype(BF16)


def merge_kernel(
    columns, parents_ref, in_ref, q_ref, nk_ref, nv_ref, rw_ref, out_ref, reward_ref, spare_ref, wide
):
    rows = in_ref.shape[1] - META
    steps, heads = q_ref.shape[1], q_ref.shape[2] // HD
    kv_heads = nk_ref.shape[2] // HD
    size = steps * heads
    column = parents_ref[0] % columns
    lane = lax.broadcasted_iota(jnp.int32, (rows, HD), 1)
    own = lane % rows == lax.broadcasted_iota(jnp.int32, (rows, HD), 0)
    own = own & (lane < 3 * rows)
    sums, tops = [], []
    for j in range(kv_heads):
        sums.append(in_ref[j * columns + column, :rows, :].astype(F32))
        tail = in_ref[j * columns + column, rows:, :].astype(F32)[0:1]
        tops.append(jnp.sum(jnp.where(own, tail, 0.0), axis=-1, keepdims=True))
        if j == 0:
            base = 3 * rows + 1
            inherited = (tail[:, base : base + 1] + tail[:, base + 1 : base + 2]) + tail[:, base + 2 : base + 3]
            spare_ref[...] = jnp.broadcast_to(inherited, spare_ref.shape)
    sum_parent = jnp.concatenate(sums, axis=0)
    top_parent = jnp.concatenate(tops, axis=0)
    for h in range(heads):
        wide[h * steps : (h + 1) * steps, :] = q_ref[0, :, h * HD : (h + 1) * HD].astype(F32)
    query = wide[...]
    step = lax.broadcasted_iota(jnp.int32, (size, 1), 0) % steps

    def spread(ref, u):
        return jnp.concatenate(
            [
                jnp.broadcast_to(ref[0, u : u + 1, k * HD : (k + 1) * HD].astype(F32), (rows, HD))
                for k in range(kv_heads)
            ],
            axis=0,
        )

    scale = HD**-0.5
    logits = [
        jnp.where(u <= step, jnp.sum(query * spread(nk_ref, u), axis=-1, keepdims=True) * scale, -1e30)
        for u in range(steps)
    ]
    top_own = functools.reduce(jnp.maximum, logits)
    weights = [jnp.exp(x - top_own) for x in logits]
    total_own = functools.reduce(jnp.add, weights)
    sum_own = functools.reduce(
        jnp.add, [w.astype(BF16).astype(F32) * spread(nv_ref, u) for u, w in enumerate(weights)]
    )
    top = jnp.maximum(top_parent, top_own)
    factor_parent = jnp.exp(top_parent - top)
    factor_own = jnp.exp(top_own - top)
    merged = (sum_parent * factor_parent + sum_own * factor_own) / (
        factor_parent + total_own * factor_own
    )
    attended = merged.astype(BF16).astype(F32)
    wide[...] = attended
    reward = jnp.zeros((steps, HD), F32)
    for h in range(heads):
        part = wide[h * steps : (h + 1) * steps, :]
        out_ref[0, :, h * HD : (h + 1) * HD] = part.astype(BF16)
        reward = reward + part * rw_ref[0:1, h * HD : (h + 1) * HD].astype(F32)
    reward_ref[...] = jnp.broadcast_to(jnp.sum(reward, axis=-1, keepdims=True), reward_ref.shape)


def per_device(
    cache_keys,
    cache_values,
    lengths,
    parent_scores,
    parents,
    queries,
    new_keys,
    new_values,
    reward_weight,
):
    columns = lax.axis_size("x")
    near, far = lax.axis_size(NEAR), lax.axis_size(FAR)
    steps, width = queries.shape[1:]
    heads = width // HD
    kv_heads = cache_keys.shape[2] // HD
    size = steps * heads
    rows = size // kv_heads
    tall = CHILDREN * rows + META

    def array(*shape, kind=BF16):
        return jax.ShapeDtypeStruct(shape, kind)

    sent = pl.pallas_call(
        functools.partial(send_kernel, columns),
        out_shape=array(near, rows + META, HD),
        in_specs=[SMEM, VMEM],
        out_specs=VMEM,
        scratch_shapes=[pltpu.VMEM((size, HD), F32)],
        compiler_params=limit(4),
        name="send",
    )(parents, queries)
    pieces = lax.all_to_all(sent, NEAR, 0, 0, tiled=True)
    turned = pl.pallas_call(
        functools.partial(turn_kernel, columns),
        out_shape=array(far, tall, HD),
        in_specs=[VMEM],
        out_specs=VMEM,
        scratch_shapes=[pltpu.SMEM((far,), jnp.int32), pltpu.VMEM((far, META, HD), F32)],
        compiler_params=limit(4),
        name="turn",
    )(pieces)
    asked = lax.all_to_all(turned, FAR, 0, 0, tiled=True)
    outputs = pl.pallas_call(
        attend_kernel,
        out_shape=array(far, tall, HD),
        in_specs=[SMEM, SMEM, VMEM, VMEM, VMEM],
        out_specs=VMEM,
        scratch_shapes=[
            pltpu.VMEM((kv_heads, CHILDREN * rows, HD), BF16),
            pltpu.VMEM((kv_heads, tall, HD), BF16),
            pltpu.SMEM((1 + CHILDREN,), jnp.int32),
        ],
        compiler_params=limit(16),
        name="attend",
    )(lengths, parent_scores, asked, cache_keys, cache_values)
    answers = lax.all_to_all(outputs, FAR, 0, 0, tiled=True)
    back = pl.pallas_call(
        functools.partial(back_kernel, columns),
        out_shape=array(near, rows + META, HD),
        in_specs=[VMEM],
        out_specs=VMEM,
        compiler_params=limit(4),
        name="back",
    )(answers)
    pieces = lax.all_to_all(back, NEAR, 0, 0, tiled=True)
    output, partial_reward, inherited = pl.pallas_call(
        functools.partial(merge_kernel, columns),
        out_shape=(
            array(*queries.shape),
            array(steps, HD, kind=F32),
            array(1, HD, kind=F32),
        ),
        in_specs=[SMEM, VMEM, VMEM, VMEM, VMEM, VMEM],
        out_specs=(VMEM, VMEM, VMEM),
        scratch_shapes=[pltpu.VMEM((size, HD), F32)],
        compiler_params=limit(4),
        name="merge",
    )(parents, pieces, queries, new_keys, new_values, reward_weight.reshape(1, width))
    reward = lax.psum(partial_reward, "tensor")[:, 0]
    score = inherited[0, :1] + jnp.sum(jax.nn.log_sigmoid(reward))
    return (output, score)


def solution(mesh):
    finer = Mesh(
        mesh.devices.reshape(mesh.shape["groups"], 4, 4, 8, mesh.shape["tensor"]),
        ("groups", "zh", "zl", "x", "tensor"),
    )
    return jax.shard_map(
        per_device,
        mesh=finer,
        in_specs=(
            P(GROUPS_DP, None, "tensor"),
            P(GROUPS_DP, None, "tensor"),
            P(GROUPS_DP),
            P(GROUPS_DP),
            P(GROUPS_DP),
            P(GROUPS_DP, None, "tensor"),
            P(GROUPS_DP, None, "tensor"),
            P(GROUPS_DP, None, "tensor"),
            P("tensor"),
        ),
        out_specs=(P(GROUPS_DP, None, "tensor"), P(GROUPS_DP)),
        check_vma=False,
    )
```

time: 188 us -> 144 us (0.77)
  blocking collectives: 103 us -> 60.3 us
  starting transfers between devices: 19.6 us -> 48.3 us
  waiting for transfers between devices: 37.5 us -> 21.9 us
  Pallas kernels: 18.8 us -> 5.58 us
    all_to_all x2, blocking collectives: 94.2 us -> 54.6 us  [the longest x1 29.3 us: per_device(): pieces = lax.all_to_all(sent, NEAR, 0, 0, tiled=True)]
    all_to_all x2, starting transfers between devices: 19.6 us -> 48.3 us  [the longest x1 37.5 us: per_device(): asked = lax.all_to_all(turned, FAR, 0, 0, tiled=True)]
    all_to_all x2, waiting for transfers between devices: 37.5 us -> 21.9 us  [the longest x1 11.6 us: per_device(): asked = lax.all_to_all(turned, FAR, 0, 0, tiled=True)]
    pallas_call x5, Pallas kernels: 18.8 us -> 5.58 us  [the longest x1 2.25 us: per_device(): pl.pallas_call(attend_kernel, out_shape=array(far, tall, HD), in_specs=[S...]
    psum x1, blocking collectives: 8.74 us -> 5.69 us  [per_device(): reward = lax.psum(partial_reward, 'tensor')[:, 0]]
where the time goes in v2:
time: 144 us
  blocking collectives  60.3 us (42%)
  starting transfers between devices  48.3 us (34%)
  waiting for transfers between devices  21.9 us (15%)
  Pallas kernels  5.58 us (4%)
  between operations  4.6 us (3%)
  local copies, waits for them, and re-layouts  2.38 us (2%)
    all_to_all x1, starting transfers between devices, per_device(): asked = lax.all_to_all(turned, FAR, 0, 0, tiled=True)  37.5 us
    all_to_all x1, blocking collectives, per_device(): pieces = lax.all_to_all(sent, NEAR, 0, 0, tiled=True)  29.3 us
    all_to_all x1, blocking collectives, per_device(): answers = lax.all_to_all(outputs, FAR, 0, 0, tiled=True)  25.3 us
    all_to_all x1, waiting for transfers between devices, per_device(): asked = lax.all_to_all(turned, FAR, 0, 0, tiled=True)  11.6 us
    all_to_all x1, starting transfers between devices, per_device(): pieces = lax.all_to_all(back, NEAR, 0, 0, tiled=True)  10.8 us
    all_to_all x1, waiting for transfers between devices, per_device(): pieces = lax.all_to_all(back, NEAR, 0, 0, tiled=True)  10.2 us
    psum x1, blocking collectives, per_device(): reward = lax.psum(partial_reward, 'tensor')[:, 0]  5.69 us
  transfers between devices with their start and end apart: 2, of which 2 were waited for; matrix products, arithmetic and copies ran while one was open for 0% of the time, Pallas kernels for 0%

profile of v2, /device:TPU:65, one launch (start us, length us, event | category | flops | bytes accessed | tf_op | source)
XLA Modules:
  0.0 143.7 jit_solution(18053549729196631929)
XLA Ops:
  0.6 0.0 copy-start
  1.4 0.0 copy-start.2
  1.4 0.7 copy-done.2
  2.2 29.3 %all_to_all.20.in_ref = bf16[32,40,128]{2,1,0:T(8,128)(2,1)S(1)} all-to-all(bf16[32,40,128]{2,1,0:T(8,128)(2,1)S(1)} %send.1), channel_id=1, replica_groups=mesh['groups'=2,'zh'=4,'zl'=4,'x'=8,'tensor'=2] {'zl','x'}, dimensions={0} | all-to-all | bytes 655360 | tf_op jit(solution)/shard_map/all_to_all | solution.py:250
  31.6 1.2 turn.1
  32.8 37.5 %all-to-all-start.1 = ((bf16[16,72,128]{2,1,0:T(8,128)(2,1)}), bf16[16,72,128]{2,1,0:T(8,128)(2,1)S(1)}, u32[]{:S(2)}, u32[]{:S(2)}) async-start(bf16[16,72,128]{2,1,0:T(8,128)(2,1)} %turn.1), calls=%async_computation.1 | async-start | bytes 589824 | tf_op jit(solution)/shard_map/all_to_all | solution.py:260
  71.5 11.6 %all-to-all-done.1.in_ref = bf16[16,72,128]{2,1,0:T(8,128)(2,1)S(1)} async-done(((bf16[16,72,128]{2,1,0:T(8,128)(2,1)}), bf16[16,72,128]{2,1,0:T(8,128)(2,1)S(1)}, u32[]{:S(2)}, u32[]{:S(2)}) %all-to-all-start.1) | async-done | bytes 294944 | tf_op jit(solution)/shard_map/all_to_all | solution.py:260
  83.2 0.0 copy-done
  83.2 0.0 copy-start.1
  83.2 1.6 %copy-done.1 = bf16[1,2048,512]{2,1,0:T(8,128)(2,1)S(1)} copy-done((bf16[1,2048,512]{2,1,0:T(8,128)(2,1)S(1)}, bf16[1,2048,512]{2,1,0:T(8,128)(2,1)}, u32[]{:S(2)}) %copy-start.1) | copy-done | bytes 2097176
  84.8 0.0 copy-start.6
  84.8 0.0 copy-start.3
  84.8 0.0 copy-start.4
  84.8 0.0 copy-start.5
  84.8 2.2 %attend.1 = bf16[16,72,128]{2,1,0:T(8,128)(2,1)S(1)} custom-call(s32[1]{0:T(128)S(6)} %copy.11.lengths_ref, f32[1]{0:T(128)S(6)} %copy.12.scores_ref, bf16[16,72,128]{2,1,0:T(8,128)(2,1)S(1)} %all-to-all-done.1.in_ref, bf16[1,2048,512]{2,1,0:T(8,128)(2,1)S(1)} %copy-done, bf16[1,2048,512]{2,1,0:T(8,128)(2,1)S(1)} %copy-done.1), custom_call_target="tpu_custom_call" | custom-call | tf_op jit(solution)/shard_map/attend/pallas_call | solution.py:261
  87.0 25.3 %all_to_all.21.in_ref = bf16[16,72,128]{2,1,0:T(8,128)(2,1)S(1)} all-to-all(bf16[16,72,128]{2,1,0:T(8,128)(2,1)S(1)} %attend.1), channel_id=1, replica_groups=mesh['groups'=2,'zh'=4,'zl'=4,'x'=8,'tensor'=2] {'zh','zl'}, dimensions={0} | all-to-all | bytes 589824 | tf_op jit(solution)/shard_map/all_to_all | solution.py:274
  112.3 1.1 back.1
  113.4 10.8 %all-to-all-start.3 = ((bf16[32,40,128]{2,1,0:T(8,128)(2,1)}), bf16[32,40,128]{2,1,0:T(8,128)(2,1)S(1)}, u32[]{:S(2)}, u32[]{:S(2)}) async-start(bf16[32,40,128]{2,1,0:T(8,128)(2,1)} %back.1), calls=%async_computation.3 | async-start | bytes 655360 | tf_op jit(solution)/shard_map/all_to_all | solution.py:283
  124.2 0.0 copy-done.6
  124.2 10.2 %all-to-all-done.3.in_ref = bf16[32,40,128]{2,1,0:T(8,128)(2,1)S(1)} async-done(((bf16[32,40,128]{2,1,0:T(8,128)(2,1)}), bf16[32,40,128]{2,1,0:T(8,128)(2,1)S(1)}, u32[]{:S(2)}, u32[]{:S(2)}) %all-to-all-start.3) | async-done | bytes 327712 | tf_op jit(solution)/shard_map/all_to_all | solution.py:283
  134.5 0.0 copy-done.3
  134.5 0.0 copy-done.4
  134.5 0.0 copy-done.5
  134.5 1.0 merge.1
  135.5 5.7 %psum.7 = f32[4,128]{1,0:T(4,128)S(1)} all-reduce(f32[4,128]{1,0:T(4,128)S(1)} %get-tuple-element.7), channel_id=1, replica_groups=mesh['groups'=2,'zh'=4,'zl'=4,'x'=8,'tensor'=2] {'tensor'}, use_global_device_ids=true, to_apply=%region_0.0 | all-reduce | flops 512 | bytes 4096 | tf_op jit(solution)/shard_map/psum | solution.py:297
  141.2 0.1 negate_reduce_fusion
  141.3 0.6 fusion
  (2 shorter events, 0.0 us)
Async XLA Ops:
  0.6 82.5 %copy-start = (bf16[1,2048,512]{2,1,0:T(8,128)(2,1)S(1)}, bf16[1,2048,512]{2,1,0:T(8,128)(2,1)}, u32[]{:S(2)}) copy-start(bf16[1,2048,512]{2,1,0:T(8,128)(2,1)} %k_ref.1) | copy-start | bytes 6291460
  1.4 0.8 copy-start.2
  32.8 50.4 %all-to-all-start.1 = ((bf16[16,72,128]{2,1,0:T(8,128)(2,1)}), bf16[16,72,128]{2,1,0:T(8,128)(2,1)S(1)}, u32[]{:S(2)}, u32[]{:S(2)}) async-start(bf16[16,72,128]{2,1,0:T(8,128)(2,1)} %turn.1), calls=%async_computation.1 | async-start | bytes 589824 | tf_op jit(solution)/shard_map/all_to_all | solution.py:260
  83.2 1.6 %copy-start.1 = (bf16[1,2048,512]{2,1,0:T(8,128)(2,1)S(1)}, bf16[1,2048,512]{2,1,0:T(8,128)(2,1)}, u32[]{:S(2)}) copy-start(bf16[1,2048,512]{2,1,0:T(8,128)(2,1)} %v_ref.1) | copy-start | bytes 6291460
  84.8 39.5 %copy-start.6 = (bf16[4096]{0:T(1024)(128)(2,1)S(1)}, bf16[4096]{0:T(1024)(128)(2,1)}, u32[]{:S(2)}) copy-start(bf16[4096]{0:T(1024)(128)(2,1)} %param.17) | copy-start | bytes 24580
  84.8 49.7 %copy-start.3 = (bf16[1,4,4096]{2,1,0:T(4,128)(2,1)S(1)}, bf16[1,4,4096]{2,1,0:T(4,128)(2,1)}, u32[]{:S(2)}) copy-start(bf16[1,4,4096]{2,1,0:T(4,128)(2,1)} %q_ref.3) | copy-start | bytes 98308
  84.8 49.7 %copy-start.4 = (bf16[1,4,512]{2,1,0:T(4,128)(2,1)S(1)}, bf16[1,4,512]{2,1,0:T(4,128)(2,1)}, u32[]{:S(2)}) copy-start(bf16[1,4,512]{2,1,0:T(4,128)(2,1)} %nk_ref.1) | copy-start | bytes 12292
  84.8 49.7 %copy-start.5 = (bf16[1,4,512]{2,1,0:T(4,128)(2,1)S(1)}, bf16[1,4,512]{2,1,0:T(4,128)(2,1)}, u32[]{:S(2)}) copy-start(bf16[1,4,512]{2,1,0:T(4,128)(2,1)} %nv_ref.1) | copy-start | bytes 12292
  113.4 21.1 %all-to-all-start.3 = ((bf16[32,40,128]{2,1,0:T(8,128)(2,1)}), bf16[32,40,128]{2,1,0:T(8,128)(2,1)S(1)}, u32[]{:S(2)}, u32[]{:S(2)}) async-start(bf16[32,40,128]{2,1,0:T(8,128)(2,1)} %back.1), calls=%async_computation.3 | async-start | bytes 655360 | tf_op jit(solution)/shard_map/all_to_all | solution.py:283

commit v3 on v2

--- a/solution.py
+++ b/solution.py
@@ -18,6 +18,7 @@
 SMEM = pl.BlockSpec(memory_space=pltpu.SMEM)
 BF16 = jnp.bfloat16
 F32 = jnp.float32
+SLOW = pl.CostEstimate(flops=10**10, bytes_accessed=2**26, transcendentals=0)
 
 
 def limit(mib):
@@ -36,7 +37,7 @@
     return [part.astype(F32) for part in (first, second, third)]
 
 
-def send_kernel(columns, parents_ref, q_ref, out_ref, item):
+def send_kernel(columns, parents_ref, lengths_ref, scores_ref, q_ref, out_ref, item):
     steps, heads = q_ref.shape[1], q_ref.shape[2] // HD
     rows = out_ref.shape[1] - META
     for h in range(heads):
@@ -211,7 +212,7 @@
     for h in range(heads):
         part = wide[h * steps : (h + 1) * steps, :]
         out_ref[0, :, h * HD : (h + 1) * HD] = part.astype(BF16)
-        reward = reward + part * rw_ref[0:1, h * HD : (h + 1) * HD].astype(F32)
+        reward = reward + part * rw_ref[h * HD : (h + 1) * HD].astype(F32)[None, :]
     reward_ref[...] = jnp.broadcast_to(jnp.sum(reward, axis=-1, keepdims=True), reward_ref.shape)
 
 
@@ -241,12 +242,13 @@
     sent = pl.pallas_call(
         functools.partial(send_kernel, columns),
         out_shape=array(near, rows + META, HD),
-        in_specs=[SMEM, VMEM],
+        in_specs=[SMEM, SMEM, SMEM, VMEM],
         out_specs=VMEM,
         scratch_shapes=[pltpu.VMEM((size, HD), F32)],
         compiler_params=limit(4),
+        cost_estimate=SLOW,
         name="send",
-    )(parents, queries)
+    )(parents, lengths, parent_scores, queries)
     pieces = lax.all_to_all(sent, NEAR, 0, 0, tiled=True)
     turned = pl.pallas_call(
         functools.partial(turn_kernel, columns),
@@ -255,6 +257,7 @@
         out_specs=VMEM,
         scratch_shapes=[pltpu.SMEM((far,), jnp.int32), pltpu.VMEM((far, META, HD), F32)],
         compiler_params=limit(4),
+        cost_estimate=SLOW,
         name="turn",
     )(pieces)
     asked = lax.all_to_all(turned, FAR, 0, 0, tiled=True)
@@ -293,7 +296,7 @@
         scratch_shapes=[pltpu.VMEM((size, HD), F32)],
         compiler_params=limit(4),
         name="merge",
-    )(parents, pieces, queries, new_keys, new_values, reward_weight.reshape(1, width))
+    )(parents, pieces, queries, new_keys, new_values, reward_weight)
     reward = lax.psum(partial_reward, "tensor")[:, 0]
     score = inherited[0, :1] + jnp.sum(jax.nn.log_sigmoid(reward))
     return (output, score)

time: 144 us -> 142 us (0.986)
  blocking collectives: 60.3 us -> 132 us
  starting transfers between devices: 48.3 us -> 0 us
  waiting for transfers between devices: 21.9 us -> 0 us
  local copies, waits for them, and re-layouts: 2.38 us -> 0.78 us
    all_to_all x0 -> x2, blocking collectives: none -> 71.2 us  [the longest x1 50.3 us: per_device(): asked = lax.all_to_all(turned, FAR, 0, 0, tiled=True)]
    all_to_all x2 -> x0, starting transfers between devices: 48.3 us -> none  [the longest x1 37.5 us: per_device(): asked = lax.all_to_all(turned, FAR, 0, 0, tiled=True)]
    all_to_all x2 -> x0, waiting for transfers between devices: 21.9 us -> none  [the longest x1 11.6 us: per_device(): asked = lax.all_to_all(turned, FAR, 0, 0, tiled=True)]
    unnamed x14, local copies, waits for them, and re-layouts: 2.36 us -> 0.78 us
  transfers between devices with their start and end apart: 2 -> 0, of which waited for: 2 -> 0; matrix products, arithmetic and copies ran while one was open for 0% -> 0% of each run, Pallas kernels for 0% -> 0%
where the time goes in v3:
time: 142 us
  blocking collectives  132 us (93%)
  between operations  4.45 us (3%)
  Pallas kernels  4.16 us (3%)
    all_to_all x1, blocking collectives, per_device(): asked = lax.all_to_all(turned, FAR, 0, 0, tiled=True)  50.3 us
    all_to_all x1, blocking collectives, per_device(): pieces = lax.all_to_all(sent, NEAR, 0, 0, tiled=True)  29.3 us
    all_to_all x1, blocking collectives, per_device(): answers = lax.all_to_all(outputs, FAR, 0, 0, tiled=True)  25.3 us
    all_to_all x1, blocking collectives, per_device(): pieces = lax.all_to_all(back, NEAR, 0, 0, tiled=True)  20.9 us
    psum x1, blocking collectives, per_device(): reward = lax.psum(partial_reward, 'tensor')[:, 0]  5.71 us

profile of v3, /device:TPU:65, one launch (start us, length us, event | category | flops | bytes accessed | tf_op | source)
XLA Modules:
  0.0 141.7 jit_solution(11241455048252782145)
XLA Ops:
  2.6 0.0 copy-start.2
  2.6 0.7 copy-done.2
  3.4 29.3 %all_to_all.20.in_ref = bf16[32,40,128]{2,1,0:T(8,128)(2,1)S(1)} all-to-all(bf16[32,40,128]{2,1,0:T(8,128)(2,1)S(1)} %send.1), channel_id=1, replica_groups=mesh['groups'=2,'zh'=4,'zl'=4,'x'=8,'tensor'=2] {'zl','x'}, dimensions={0} | all-to-all | bytes 655360 | tf_op jit(solution)/shard_map/all_to_all | solution.py:252
  32.7 0.0 copy-start
  32.7 0.0 copy-start.1
  32.7 0.5 turn.1
  33.2 50.3 %all_to_all.21.in_ref = bf16[16,72,128]{2,1,0:T(8,128)(2,1)S(1)} all-to-all(bf16[16,72,128]{2,1,0:T(8,128)(2,1)S(1)} %turn.1), channel_id=1, replica_groups=mesh['groups'=2,'zh'=4,'zl'=4,'x'=8,'tensor'=2] {'zh','zl'}, dimensions={0} | all-to-all | bytes 589824 | tf_op jit(solution)/shard_map/all_to_all | solution.py:263
  83.5 0.0 copy-done
  83.5 0.0 copy-done.1
  83.5 0.0 copy-start.3
  83.5 0.0 copy-start.4
  83.5 0.0 copy-start.5
  83.6 0.0 copy-start.6
  83.6 2.2 %attend.1 = bf16[16,72,128]{2,1,0:T(8,128)(2,1)S(1)} custom-call(s32[1]{0:T(128)S(6)} %copy.11.lengths_ref, f32[1]{0:T(128)S(6)} %copy.12.scores_ref, bf16[16,72,128]{2,1,0:T(8,128)(2,1)S(1)} %all_to_all.21.in_ref, bf16[1,2048,512]{2,1,0:T(8,128)(2,1)S(1)} %copy-done, bf16[1,2048,512]{2,1,0:T(8,128)(2,1)S(1)} %copy-done.1), custom_call_target="tpu_custom_call" | custom-call | tf_op jit(solution)/shard_map/attend/pallas_call | solution.py:264
  85.8 25.3 %all_to_all.22.in_ref = bf16[16,72,128]{2,1,0:T(8,128)(2,1)S(1)} all-to-all(bf16[16,72,128]{2,1,0:T(8,128)(2,1)S(1)} %attend.1), channel_id=1, replica_groups=mesh['groups'=2,'zh'=4,'zl'=4,'x'=8,'tensor'=2] {'zh','zl'}, dimensions={0} | all-to-all | bytes 589824 | tf_op jit(solution)/shard_map/all_to_all | solution.py:277
  111.1 0.4 back.1
  111.5 20.9 %all_to_all.23.in_ref = bf16[32,40,128]{2,1,0:T(8,128)(2,1)S(1)} all-to-all(bf16[32,40,128]{2,1,0:T(8,128)(2,1)S(1)} %back.1), channel_id=1, replica_groups=mesh['groups'=2,'zh'=4,'zl'=4,'x'=8,'tensor'=2] {'zl','x'}, dimensions={0} | all-to-all | bytes 655360 | tf_op jit(solution)/shard_map/all_to_all | solution.py:286
  132.4 0.0 copy-done.3
  132.4 0.0 copy-done.4
  132.4 0.0 copy-done.5
  132.4 0.0 copy-done.6
  132.4 1.0 merge.1
  133.4 5.7 %psum.7 = f32[4,128]{1,0:T(4,128)S(1)} all-reduce(f32[4,128]{1,0:T(4,128)S(1)} %get-tuple-element.7), channel_id=1, replica_groups=mesh['groups'=2,'zh'=4,'zl'=4,'x'=8,'tensor'=2] {'tensor'}, use_global_device_ids=true, to_apply=%region_0.0 | all-reduce | flops 512 | bytes 4096 | tf_op jit(solution)/shard_map/psum | solution.py:300
  139.1 0.1 negate_reduce_fusion
  139.2 0.6 fusion
  (1 shorter events, 0.0 us)
Async XLA Ops:
  2.6 0.8 copy-start.2
  32.7 50.8 %copy-start = (bf16[1,2048,512]{2,1,0:T(8,128)(2,1)S(1)}, bf16[1,2048,512]{2,1,0:T(8,128)(2,1)}, u32[]{:S(2)}) copy-start(bf16[1,2048,512]{2,1,0:T(8,128)(2,1)} %k_ref.1) | copy-start | bytes 6291460
  32.7 50.8 %copy-start.1 = (bf16[1,2048,512]{2,1,0:T(8,128)(2,1)S(1)}, bf16[1,2048,512]{2,1,0:T(8,128)(2,1)}, u32[]{:S(2)}) copy-start(bf16[1,2048,512]{2,1,0:T(8,128)(2,1)} %v_ref.1) | copy-start | bytes 6291460
  83.5 48.9 %copy-start.3 = (bf16[1,4,4096]{2,1,0:T(4,128)(2,1)S(1)}, bf16[1,4,4096]{2,1,0:T(4,128)(2,1)}, u32[]{:S(2)}) copy-start(bf16[1,4,4096]{2,1,0:T(4,128)(2,1)} %q_ref.3) | copy-start | bytes 98308
  83.5 48.9 %copy-start.4 = (bf16[4096]{0:T(1024)(128)(2,1)S(1)}, bf16[4096]{0:T(1024)(128)(2,1)}, u32[]{:S(2)}) copy-start(bf16[4096]{0:T(1024)(128)(2,1)} %rw_ref.1) | copy-start | bytes 24580
  83.5 48.9 %copy-start.5 = (bf16[1,4,512]{2,1,0:T(4,128)(2,1)S(1)}, bf16[1,4,512]{2,1,0:T(4,128)(2,1)}, u32[]{:S(2)}) copy-start(bf16[1,4,512]{2,1,0:T(4,128)(2,1)} %nk_ref.1) | copy-start | bytes 12292
  83.6 48.9 %copy-start.6 = (bf16[1,4,512]{2,1,0:T(4,128)(2,1)S(1)}, bf16[1,4,512]{2,1,0:T(4,128)(2,1)}, u32[]{:S(2)}) copy-start(bf16[1,4,512]{2,1,0:T(4,128)(2,1)} %nv_ref.1) | copy-start | bytes 12292

commit v4 on v3

--- a/solution.py
+++ b/solution.py
@@ -10,7 +10,8 @@
 
 HD = 128
 CHILDREN = 2
-META = 8
+PAIR = 2
+TILE = 8
 GROUPS_DP = ("groups", "zh", "zl", "x")
 NEAR = ("zl", "x")
 FAR = ("zh", "zl")
@@ -37,25 +38,30 @@
     return [part.astype(F32) for part in (first, second, third)]
 
 
-def send_kernel(columns, parents_ref, lengths_ref, scores_ref, q_ref, out_ref, item):
-    steps, heads = q_ref.shape[1], q_ref.shape[2] // HD
-    rows = out_ref.shape[1] - META
-    for h in range(heads):
-        item[h * steps : (h + 1) * steps, :] = q_ref[0, :, h * HD : (h + 1) * HD].astype(F32)
-    parent = jnp.full((META, HD), parents_ref[0].astype(F32), F32).astype(BF16)
+def send_kernel(columns, parents_ref, lengths_ref, scores_ref, q_ref, out_ref, facts_ref):
+    steps = q_ref.shape[1]
+    pairs = out_ref.shape[1] - 1
+    turns = steps // PAIR
+    facts = [parents_ref[0].astype(F32), lengths_ref[0].astype(F32), scores_ref[0]]
+    for n, fact in enumerate(facts):
+        facts_ref[n : n + 1, :] = jnp.full((1, HD), fact, F32)
+    parent = jnp.full((PAIR, HD), facts[0], F32).astype(BF16)
     for j in range(out_ref.shape[0] // columns):
-        piece = item[j * rows : (j + 1) * rows, :].astype(BF16)
+        for g in range(pairs):
+            h, t = j * (pairs // turns) + g // turns, g % turns * PAIR
+            pair = q_ref[0, t : t + PAIR, h * HD : (h + 1) * HD]
+            for d in range(columns):
+                out_ref[j * columns + d, g] = pair
         for d in range(columns):
-            out_ref[j * columns + d, :rows, :] = piece
-            out_ref[j * columns + d, rows:, :] = parent
+            out_ref[j * columns + d, pairs] = parent
 
 
 def turn_kernel(columns, in_ref, out_ref, used, meta):
-    rows = in_ref.shape[1] - META
+    pairs = in_ref.shape[1] - 1
     block = in_ref.shape[0] // columns
     first = lax.axis_index("zh") * block
     mine = lax.axis_index("x")
-    parents = [whole_number(in_ref[i, rows:, :].astype(F32)[0:1], 0) for i in range(in_ref.shape[0])]
+    parents = [whole_number(in_ref[i, pairs].astype(F32)[0:1], 0) for i in range(in_ref.shape[0])]
     meta[...] = jnp.full(meta.shape, -1.0, F32)
     for i in range(out_ref.shape[0]):
         used[i] = 0
@@ -66,22 +72,23 @@
             row = parent // columns
             place = used[row]
             used[row] = place + 1
-            out_ref[row, pl.ds(pl.multiple_of(place * rows, rows), rows), :] = in_ref[i, :rows, :]
+            out_ref[row, pl.ds(place * pairs, pairs)] = in_ref[i, :pairs]
             child = first * columns + i
             meta[row, pl.ds(place, 1), :] = jnp.full((1, HD), child.astype(F32), F32)
 
     for i in range(out_ref.shape[0]):
-        out_ref[i, CHILDREN * rows :, :] = meta[i].astype(BF16)
-
-
-def attend_kernel(lengths_ref, scores_ref, in_ref, k_ref, v_ref, out_ref, q, item, found):
-    kv_heads, tall = item.shape[:2]
-    rows = (tall - META) // CHILDREN
+        out_ref[i, CHILDREN * pairs] = meta[i, :CHILDREN, :].astype(BF16)
+
+
+def attend_kernel(facts_ref, in_ref, k_ref, v_ref, out_ref, q, result, item, found):
+    kv_heads = item.shape[0]
+    pairs = in_ref.shape[1] // CHILDREN
+    rows = pairs * PAIR
     context = k_ref.shape[1]
     blocks = in_ref.shape[0] // kv_heads
     ids = []
     for b in range(blocks):
-        tail = in_ref[b * kv_heads, CHILDREN * rows :, :].astype(F32)
+        tail = in_ref[b * kv_heads, CHILDREN * pairs].astype(F32)
         ids.append([whole_number(tail[c : c + 1], 0) for c in range(CHILDREN)])
     q[...] = jnp.zeros_like(q)
     found[0] = 0
@@ -96,20 +103,23 @@
                 found[0] = n + 1
                 found[1 + n] = ids[b][c]
                 for j in range(kv_heads):
-                    piece = in_ref[b * kv_heads + j, c * rows : (c + 1) * rows, :]
-                    q[j, pl.ds(pl.multiple_of(n * rows, rows), rows), :] = piece
+                    for g in range(pairs):
+                        pair = in_ref[b * kv_heads + j, c * pairs + g].astype(F32)
+                        q[j, n, g * PAIR : (g + 1) * PAIR, :] = pair
 
     scale = HD**-0.5
-    valid = lax.broadcasted_iota(jnp.int32, (CHILDREN * rows, context), 1) < lengths_ref[0]
+    length = facts_ref[1:2, 0:1].astype(jnp.int32)
+    valid = lax.broadcasted_iota(jnp.int32, (CHILDREN * rows, context), 1) < length
     lane = lax.broadcasted_iota(jnp.int32, (rows, HD), 1)
     diagonal = lane % rows == lax.broadcasted_iota(jnp.int32, (rows, HD), 0)
     part = lax.broadcasted_iota(jnp.int32, (1, HD), 1)
-    score = in_parts(jnp.full((1, HD), scores_ref[0], F32))
+    score = in_parts(facts_ref[2:3, :])
     for j in range(kv_heads):
         keys = k_ref[0, :, j * HD : (j + 1) * HD]
         values = v_ref[0, :, j * HD : (j + 1) * HD]
+        query = q[j].reshape(CHILDREN * rows, HD).astype(BF16)
         logits = (
-            lax.dot_general(q[j], keys, (((1,), (1,)), ((), ())), preferred_element_type=F32)
+            lax.dot_general(query, keys, (((1,), (1,)), ((), ())), preferred_element_type=F32)
             * scale
         )
         logits = jnp.where(valid, logits, -1e30)
@@ -117,7 +127,9 @@
         weights = jnp.exp(logits - top)
         total = jnp.sum(weights, axis=-1, keepdims=True)
         summed = jnp.dot(weights.astype(BF16), values, preferred_element_type=F32)
-        item[j, : CHILDREN * rows, :] = (summed / total).astype(BF16)
+        result[...] = summed / total
+        for g in range(CHILDREN * pairs):
+            item[j, g] = result[g * PAIR : (g + 1) * PAIR, :].astype(BF16)
         log_total = top + jnp.log(total)
         tails = []
         for c in range(CHILDREN):
@@ -129,18 +141,18 @@
             for n, extra in enumerate([jnp.full((1, HD), found[1 + c].astype(F32), F32), *score]):
                 line = jnp.where(part == 3 * rows + n, extra, line)
             tails.append(line)
-        tails.append(jnp.zeros((META - CHILDREN, HD), F32))
-        item[j, CHILDREN * rows :, :] = jnp.concatenate(tails, axis=0).astype(BF16)
+        item[j, CHILDREN * pairs] = jnp.concatenate(tails, axis=0).astype(BF16)
     for b in range(blocks):
         out_ref[b * kv_heads : (b + 1) * kv_heads] = item[...]
 
 
 def back_kernel(columns, in_ref, out_ref):
-    rows = out_ref.shape[1] - META
+    pairs = out_ref.shape[1] - 1
+    rows = pairs * PAIR
     first = lax.axis_index("zh") * out_ref.shape[0]
     children = []
     for i in range(in_ref.shape[0]):
-        tail = in_ref[i, CHILDREN * rows :, :].astype(F32)
+        tail = in_ref[i, CHILDREN * pairs].astype(F32)
         children.append([whole_number(tail[c : c + 1], 3 * rows) for c in range(CHILDREN)])
     for i in range(in_ref.shape[0]):
         for c in range(CHILDREN):
@@ -148,32 +160,34 @@
 
             @pl.when((place >= 0) & (place < out_ref.shape[0]))
             def _():
-                out_ref[place, :rows, :] = in_ref[i, c * rows : (c + 1) * rows, :]
-                tail = in_ref[i, CHILDREN * rows :, :].astype(F32)[c : c + 1]
-                out_ref[place, rows:, :] = jnp.broadcast_to(tail, (META, HD)).astype(BF16)
+                out_ref[place, :pairs] = in_ref[i, c * pairs : (c + 1) * pairs]
+                tail = in_ref[i, CHILDREN * pairs].astype(F32)[c : c + 1]
+                out_ref[place, pairs] = jnp.broadcast_to(tail, (PAIR, HD)).astype(BF16)
 
 
 def merge_kernel(
-    columns, parents_ref, in_ref, q_ref, nk_ref, nv_ref, rw_ref, out_ref, reward_ref, spare_ref, wide
+    columns, facts_ref, in_ref, q_ref, nk_ref, nv_ref, rw_ref, out_ref, reward_ref, spare_ref, wide, came
 ):
-    rows = in_ref.shape[1] - META
+    pairs = in_ref.shape[1] - 1
+    rows = pairs * PAIR
     steps, heads = q_ref.shape[1], q_ref.shape[2] // HD
     kv_heads = nk_ref.shape[2] // HD
     size = steps * heads
-    column = parents_ref[0] % columns
+    column = whole_number(facts_ref[0:1, :], 0) % columns
     lane = lax.broadcasted_iota(jnp.int32, (rows, HD), 1)
     own = lane % rows == lax.broadcasted_iota(jnp.int32, (rows, HD), 0)
     own = own & (lane < 3 * rows)
-    sums, tops = [], []
+    tops = []
     for j in range(kv_heads):
-        sums.append(in_ref[j * columns + column, :rows, :].astype(F32))
-        tail = in_ref[j * columns + column, rows:, :].astype(F32)[0:1]
+        for g in range(pairs):
+            came[j * rows + g * PAIR : j * rows + (g + 1) * PAIR, :] = in_ref[j * columns + column, g].astype(F32)
+        tail = in_ref[j * columns + column, pairs].astype(F32)[0:1]
         tops.append(jnp.sum(jnp.where(own, tail, 0.0), axis=-1, keepdims=True))
         if j == 0:
             base = 3 * rows + 1
             inherited = (tail[:, base : base + 1] + tail[:, base + 1 : base + 2]) + tail[:, base + 2 : base + 3]
             spare_ref[...] = jnp.broadcast_to(inherited, spare_ref.shape)
-    sum_parent = jnp.concatenate(sums, axis=0)
+    sum_parent = came[...]
     top_parent = jnp.concatenate(tops, axis=0)
     for h in range(heads):
         wide[h * steps : (h + 1) * steps, :] = q_ref[0, :, h * HD : (h + 1) * HD].astype(F32)
@@ -234,17 +248,17 @@
     kv_heads = cache_keys.shape[2] // HD
     size = steps * heads
     rows = size // kv_heads
-    tall = CHILDREN * rows + META
+    pairs = rows // PAIR
+    one, both = (pairs + 1, PAIR, HD), (CHILDREN * pairs + 1, PAIR, HD)
 
     def array(*shape, kind=BF16):
         return jax.ShapeDtypeStruct(shape, kind)
 
-    sent = pl.pallas_call(
+    sent, facts = pl.pallas_call(
         functools.partial(send_kernel, columns),
-        out_shape=array(near, rows + META, HD),
+        out_shape=(array(near, *one), array(TILE, HD, kind=F32)),
         in_specs=[SMEM, SMEM, SMEM, VMEM],
-        out_specs=VMEM,
-        scratch_shapes=[pltpu.VMEM((size, HD), F32)],
+        out_specs=(VMEM, VMEM),
         compiler_params=limit(4),
         cost_estimate=SLOW,
         name="send",
@@ -252,10 +266,10 @@
     pieces = lax.all_to_all(sent, NEAR, 0, 0, tiled=True)
     turned = pl.pallas_call(
         functools.partial(turn_kernel, columns),
-        out_shape=array(far, tall, HD),
+        out_shape=array(far, *both),
         in_specs=[VMEM],
         out_specs=VMEM,
-        scratch_shapes=[pltpu.SMEM((far,), jnp.int32), pltpu.VMEM((far, META, HD), F32)],
+        scratch_shapes=[pltpu.SMEM((far,), jnp.int32), pltpu.VMEM((far, TILE, HD), F32)],
         compiler_params=limit(4),
         cost_estimate=SLOW,
         name="turn",
@@ -263,21 +277,22 @@
     asked = lax.all_to_all(turned, FAR, 0, 0, tiled=True)
     outputs = pl.pallas_call(
         attend_kernel,
-        out_shape=array(far, tall, HD),
-        in_specs=[SMEM, SMEM, VMEM, VMEM, VMEM],
+        out_shape=array(far, *both),
+        in_specs=[VMEM, VMEM, VMEM, VMEM],
         out_specs=VMEM,
         scratch_shapes=[
-            pltpu.VMEM((kv_heads, CHILDREN * rows, HD), BF16),
-            pltpu.VMEM((kv_heads, tall, HD), BF16),
+            pltpu.VMEM((kv_heads, CHILDREN, rows, HD), F32),
+            pltpu.VMEM((CHILDREN * rows, HD), F32),
+            pltpu.VMEM((kv_heads, *both), BF16),
             pltpu.SMEM((1 + CHILDREN,), jnp.int32),
         ],
         compiler_params=limit(16),
         name="attend",
-    )(lengths, parent_scores, asked, cache_keys, cache_values)
+    )(facts, asked, cache_keys, cache_values)
     answers = lax.all_to_all(outputs, FAR, 0, 0, tiled=True)
     back = pl.pallas_call(
         functools.partial(back_kernel, columns),
-        out_shape=array(near, rows + META, HD),
+        out_shape=array(near, *one),
         in_specs=[VMEM],
         out_specs=VMEM,
         compiler_params=limit(4),
@@ -291,12 +306,12 @@
             array(steps, HD, kind=F32),
             array(1, HD, kind=F32),
         ),
-        in_specs=[SMEM, VMEM, VMEM, VMEM, VMEM, VMEM],
+        in_specs=[VMEM, VMEM, VMEM, VMEM, VMEM, VMEM],
         out_specs=(VMEM, VMEM, VMEM),
-        scratch_shapes=[pltpu.VMEM((size, HD), F32)],
+        scratch_shapes=[pltpu.VMEM((size, HD), F32), pltpu.VMEM((size, HD), F32)],
         compiler_params=limit(4),
         name="merge",
-    )(parents, pieces, queries, new_keys, new_values, reward_weight)
+    )(facts, pieces, queries, new_keys, new_values, reward_weight)
     reward = lax.psum(partial_reward, "tensor")[:, 0]
     score = inherited[0, :1] + jnp.sum(jax.nn.log_sigmoid(reward))
     return (output, score)

time: 142 us -> 139 us (0.979)
  blocking collectives: 132 us -> 128 us
    all_to_all x1, blocking collectives: 25.3 us -> 23.2 us  [per_device(): answers = lax.all_to_all(outputs, FAR, 0, 0, tiled=True)]
    all_to_all x1, blocking collectives: 50.3 us -> 48.8 us  [per_device(): asked = lax.all_to_all(turned, FAR, 0, 0, tiled=True)]
where the time goes in v4:
time: 139 us
  blocking collectives  128 us (92%)
  Pallas kernels  4.57 us (3%)
  between operations  4.45 us (3%)
    all_to_all x1, blocking collectives, per_device(): asked = lax.all_to_all(turned, FAR, 0, 0, tiled=True)  48.8 us
    all_to_all x1, blocking collectives, per_device(): pieces = lax.all_to_all(sent, NEAR, 0, 0, tiled=True)  29 us
    all_to_all x1, blocking collectives, per_device(): answers = lax.all_to_all(outputs, FAR, 0, 0, tiled=True)  23.2 us
    all_to_all x1, blocking collectives, per_device(): pieces = lax.all_to_all(back, NEAR, 0, 0, tiled=True)  21 us
    psum x1, blocking collectives, per_device(): reward = lax.psum(partial_reward, 'tensor')[:, 0]  6.02 us

profile of v4, /device:TPU:65, one launch (start us, length us, event | category | flops | bytes accessed | tf_op | source)
XLA Modules:
  0.0 138.5 jit_solution(10123642295069342501)
XLA Ops:
  2.6 0.0 copy-start.2
  2.6 0.7 copy-done.2
  3.3 0.2 send.1
  3.5 29.0 %all_to_all.20.in_ref = bf16[32,17,2,128]{3,2,1,0:T(2,128)(2,1)S(1)} all-to-all(bf16[32,17,2,128]{3,2,1,0:T(2,128)(2,1)S(1)} %get-tuple-element.8), channel_id=1, replica_groups=mesh['groups'=2,'zh'=4,'zl'=4,'x'=8,'tensor'=2] {'zl','x'}, dimensions={0} | all-to-all | bytes 557056 | tf_op jit(solution)/shard_map/all_to_all | solution.py:266
  32.5 0.0 copy-start
  32.5 0.0 copy-start.1
  32.5 0.5 turn.1
  33.0 48.8 %all_to_all.21.in_ref = bf16[16,33,2,128]{3,2,1,0:T(2,128)(2,1)S(1)} all-to-all(bf16[16,33,2,128]{3,2,1,0:T(2,128)(2,1)S(1)} %turn.1), channel_id=1, replica_groups=mesh['groups'=2,'zh'=4,'zl'=4,'x'=8,'tensor'=2] {'zh','zl'}, dimensions={0} | all-to-all | bytes 540672 | tf_op jit(solution)/shard_map/all_to_all | solution.py:277
  81.8 0.0 copy-done
  81.8 0.0 copy-done.1
  81.8 0.0 copy-start.3
  81.8 0.0 copy-start.4
  81.8 0.0 copy-start.5
  81.8 0.0 copy-start.6
  81.8 2.5 %attend.1 = bf16[16,33,2,128]{3,2,1,0:T(2,128)(2,1)S(1)} custom-call(f32[8,128]{1,0:T(8,128)S(1)} %get-tuple-element.7.facts_ref, bf16[16,33,2,128]{3,2,1,0:T(2,128)(2,1)S(1)} %all_to_all.21.in_ref, bf16[1,2048,512]{2,1,0:T(8,128)(2,1)S(1)} %copy-done, bf16[1,2048,512]{2,1,0:T(8,128)(2,1)S(1)} %copy-done.1), custom_call_target="tpu_custom_call" | custom-call | tf_op jit(solution)/shard_map/attend/pallas_call | solution.py:278
  84.3 23.2 %all_to_all.22.in_ref = bf16[16,33,2,128]{3,2,1,0:T(2,128)(2,1)S(1)} all-to-all(bf16[16,33,2,128]{3,2,1,0:T(2,128)(2,1)S(1)} %attend.1), channel_id=1, replica_groups=mesh['groups'=2,'zh'=4,'zl'=4,'x'=8,'tensor'=2] {'zh','zl'}, dimensions={0} | all-to-all | bytes 540672 | tf_op jit(solution)/shard_map/all_to_all | solution.py:292
  107.5 0.4 back.1
  107.9 21.0 %all_to_all.23.in_ref = bf16[32,17,2,128]{3,2,1,0:T(2,128)(2,1)S(1)} all-to-all(bf16[32,17,2,128]{3,2,1,0:T(2,128)(2,1)S(1)} %back.1), channel_id=1, replica_groups=mesh['groups'=2,'zh'=4,'zl'=4,'x'=8,'tensor'=2] {'zl','x'}, dimensions={0} | all-to-all | bytes 557056 | tf_op jit(solution)/shard_map/all_to_all | solution.py:301
  128.9 0.0 copy-done.3
  128.9 0.0 copy-done.4
  128.9 0.0 copy-done.5
  128.9 0.0 copy-done.6
  128.9 1.0 merge.1
  130.0 6.0 %psum.7 = f32[4,128]{1,0:T(4,128)S(1)} all-reduce(f32[4,128]{1,0:T(4,128)S(1)} %get-tuple-element.11), channel_id=1, replica_groups=mesh['groups'=2,'zh'=4,'zl'=4,'x'=8,'tensor'=2] {'tensor'}, use_global_device_ids=true, to_apply=%region_0.0 | all-reduce | flops 512 | bytes 4096 | tf_op jit(solution)/shard_map/psum | solution.py:315
  136.0 0.1 negate_reduce_fusion
  136.1 0.6 fusion
Async XLA Ops:
  2.6 0.8 copy-start.2
  32.5 49.4 %copy-start = (bf16[1,2048,512]{2,1,0:T(8,128)(2,1)S(1)}, bf16[1,2048,512]{2,1,0:T(8,128)(2,1)}, u32[]{:S(2)}) copy-start(bf16[1,2048,512]{2,1,0:T(8,128)(2,1)} %k_ref.1) | copy-start | bytes 6291460
  32.5 49.4 %copy-start.1 = (bf16[1,2048,512]{2,1,0:T(8,128)(2,1)S(1)}, bf16[1,2048,512]{2,1,0:T(8,128)(2,1)}, u32[]{:S(2)}) copy-start(bf16[1,2048,512]{2,1,0:T(8,128)(2,1)} %v_ref.1) | copy-start | bytes 6291460
  81.8 47.1 %copy-start.3 = (bf16[1,4,4096]{2,1,0:T(4,128)(2,1)S(1)}, bf16[1,4,4096]{2,1,0:T(4,128)(2,1)}, u32[]{:S(2)}) copy-start(bf16[1,4,4096]{2,1,0:T(4,128)(2,1)} %q_ref.3) | copy-start | bytes 98308
  81.8 47.1 %copy-start.4 = (bf16[4096]{0:T(1024)(128)(2,1)S(1)}, bf16[4096]{0:T(1024)(128)(2,1)}, u32[]{:S(2)}) copy-start(bf16[4096]{0:T(1024)(128)(2,1)} %rw_ref.1) | copy-start | bytes 24580
  81.8 47.1 %copy-start.5 = (bf16[1,4,512]{2,1,0:T(4,128)(2,1)S(1)}, bf16[1,4,512]{2,1,0:T(4,128)(2,1)}, u32[]{:S(2)}) copy-start(bf16[1,4,512]{2,1,0:T(4,128)(2,1)} %nk_ref.1) | copy-start | bytes 12292
  81.8 47.1 %copy-start.6 = (bf16[1,4,512]{2,1,0:T(4,128)(2,1)S(1)}, bf16[1,4,512]{2,1,0:T(4,128)(2,1)}, u32[]{:S(2)}) copy-start(bf16[1,4,512]{2,1,0:T(4,128)(2,1)} %nv_ref.1) | copy-start | bytes 12292

commit v5 on v4

--- a/solution.py
+++ b/solution.py
@@ -38,7 +38,7 @@
     return [part.astype(F32) for part in (first, second, third)]
 
 
-def send_kernel(columns, parents_ref, lengths_ref, scores_ref, q_ref, out_ref, facts_ref):
+def send_kernel(kv_heads, parents_ref, lengths_ref, scores_ref, q_ref, out_ref, facts_ref):
     steps = q_ref.shape[1]
     pairs = out_ref.shape[1] - 1
     turns = steps // PAIR
@@ -46,35 +46,34 @@
     for n, fact in enumerate(facts):
         facts_ref[n : n + 1, :] = jnp.full((1, HD), fact, F32)
     parent = jnp.full((PAIR, HD), facts[0], F32).astype(BF16)
-    for j in range(out_ref.shape[0] // columns):
+    for j in range(kv_heads):
         for g in range(pairs):
             h, t = j * (pairs // turns) + g // turns, g % turns * PAIR
             pair = q_ref[0, t : t + PAIR, h * HD : (h + 1) * HD]
-            for d in range(columns):
-                out_ref[j * columns + d, g] = pair
-        for d in range(columns):
-            out_ref[j * columns + d, pairs] = parent
+            for d in range(j, out_ref.shape[0], kv_heads):
+                out_ref[d, g] = pair
+        for d in range(j, out_ref.shape[0], kv_heads):
+            out_ref[d, pairs] = parent
 
 
 def turn_kernel(columns, in_ref, out_ref, used, meta):
     pairs = in_ref.shape[1] - 1
-    block = in_ref.shape[0] // columns
-    first = lax.axis_index("zh") * block
+    first = lax.axis_index("zh") * out_ref.shape[0]
     mine = lax.axis_index("x")
     parents = [whole_number(in_ref[i, pairs].astype(F32)[0:1], 0) for i in range(in_ref.shape[0])]
     meta[...] = jnp.full(meta.shape, -1.0, F32)
     for i in range(out_ref.shape[0]):
         used[i] = 0
     for i, parent in enumerate(parents):
-
-        @pl.when(parent % columns == mine)
+        place = parent - first
+
+        @pl.when((place >= 0) & (place < out_ref.shape[0]))
         def _():
-            row = parent // columns
-            place = used[row]
-            used[row] = place + 1
-            out_ref[row, pl.ds(place * pairs, pairs)] = in_ref[i, :pairs]
-            child = first * columns + i
-            meta[row, pl.ds(place, 1), :] = jnp.full((1, HD), child.astype(F32), F32)
+            n = used[place]
+            used[place] = n + 1
+            out_ref[place, pl.ds(n * pairs, pairs)] = in_ref[i, :pairs]
+            child = i * columns + mine
+            meta[place, pl.ds(n, 1), :] = jnp.full((1, HD), child.astype(F32), F32)
 
     for i in range(out_ref.shape[0]):
         out_ref[i, CHILDREN * pairs] = meta[i, :CHILDREN, :].astype(BF16)
@@ -85,16 +84,16 @@
     pairs = in_ref.shape[1] // CHILDREN
     rows = pairs * PAIR
     context = k_ref.shape[1]
-    blocks = in_ref.shape[0] // kv_heads
+    columns = in_ref.shape[0] // kv_heads
     ids = []
-    for b in range(blocks):
-        tail = in_ref[b * kv_heads, CHILDREN * pairs].astype(F32)
+    for b in range(columns):
+        tail = in_ref[b, CHILDREN * pairs].astype(F32)
         ids.append([whole_number(tail[c : c + 1], 0) for c in range(CHILDREN)])
     q[...] = jnp.zeros_like(q)
     found[0] = 0
     for c in range(CHILDREN):
         found[1 + c] = -1
-    for b in range(blocks):
+    for b in range(columns):
         for c in range(CHILDREN):
 
             @pl.when(ids[b][c] >= 0)
@@ -104,7 +103,7 @@
                 found[1 + n] = ids[b][c]
                 for j in range(kv_heads):
                     for g in range(pairs):
-                        pair = in_ref[b * kv_heads + j, c * pairs + g].astype(F32)
+                        pair = in_ref[j * columns + b, c * pairs + g].astype(F32)
                         q[j, n, g * PAIR : (g + 1) * PAIR, :] = pair
 
     scale = HD**-0.5
@@ -142,7 +141,7 @@
                 line = jnp.where(part == 3 * rows + n, extra, line)
             tails.append(line)
         item[j, CHILDREN * pairs] = jnp.concatenate(tails, axis=0).astype(BF16)
-    for b in range(blocks):
+    for b in range(out_ref.shape[0] // kv_heads):
         out_ref[b * kv_heads : (b + 1) * kv_heads] = item[...]
 
 
@@ -255,26 +254,26 @@
         return jax.ShapeDtypeStruct(shape, kind)
 
     sent, facts = pl.pallas_call(
-        functools.partial(send_kernel, columns),
-        out_shape=(array(near, *one), array(TILE, HD, kind=F32)),
+        functools.partial(send_kernel, kv_heads),
+        out_shape=(array(far, *one), array(TILE, HD, kind=F32)),
         in_specs=[SMEM, SMEM, SMEM, VMEM],
         out_specs=(VMEM, VMEM),
         compiler_params=limit(4),
         cost_estimate=SLOW,
         name="send",
     )(parents, lengths, parent_scores, queries)
-    pieces = lax.all_to_all(sent, NEAR, 0, 0, tiled=True)
+    pieces = lax.all_to_all(sent, FAR, 0, 0, tiled=True)
     turned = pl.pallas_call(
         functools.partial(turn_kernel, columns),
-        out_shape=array(far, *both),
+        out_shape=array(near, *both),
         in_specs=[VMEM],
         out_specs=VMEM,
-        scratch_shapes=[pltpu.SMEM((far,), jnp.int32), pltpu.VMEM((far, TILE, HD), F32)],
+        scratch_shapes=[pltpu.SMEM((near,), jnp.int32), pltpu.VMEM((near, TILE, HD), F32)],
         compiler_params=limit(4),
         cost_estimate=SLOW,
         name="turn",
     )(pieces)
-    asked = lax.all_to_all(turned, FAR, 0, 0, tiled=True)
+    asked = lax.all_to_all(turned, NEAR, 0, 0, tiled=True)
     outputs = pl.pallas_call(
         attend_kernel,
         out_shape=array(far, *both),

time: 139 us -> 139 us (level)
    all_to_all x2, blocking collectives: 77.8 us -> 80.6 us  [the longest x1 55.8 us: per_device(): pieces = lax.all_to_all(sent, FAR, 0, 0, tiled=True)]
where the time goes in v5:
time: 139 us
  blocking collectives  129 us (93%)
  between operations  4.45 us (3%)
  Pallas kernels  4.25 us (3%)
    all_to_all x1, blocking collectives, per_device(): pieces = lax.all_to_all(sent, FAR, 0, 0, tiled=True)  55.8 us
    all_to_all x1, blocking collectives, per_device(): asked = lax.all_to_all(turned, NEAR, 0, 0, tiled=True)  24.7 us
    all_to_all x1, blocking collectives, per_device(): answers = lax.all_to_all(outputs, FAR, 0, 0, tiled=True)  22 us
    all_to_all x1, blocking collectives, per_device(): pieces = lax.all_to_all(back, NEAR, 0, 0, tiled=True)  20.3 us
    psum x1, blocking collectives, per_device(): reward = lax.psum(partial_reward, 'tensor')[:, 0]  5.9 us

profile of v5, /device:TPU:65, one launch (start us, length us, event | category | flops | bytes accessed | tf_op | source)
XLA Modules:
  0.0 139.1 jit_solution(10847213129296824592)
XLA Ops:
  2.6 0.0 copy-start.2
  2.6 0.7 copy-done.2
  3.3 0.1 send.1
  3.4 55.8 %all_to_all.20.in_ref = bf16[16,17,2,128]{3,2,1,0:T(2,128)(2,1)S(1)} all-to-all(bf16[16,17,2,128]{3,2,1,0:T(2,128)(2,1)S(1)} %get-tuple-element.8), channel_id=1, replica_groups=mesh['groups'=2,'zh'=4,'zl'=4,'x'=8,'tensor'=2] {'zh','zl'}, dimensions={0} | all-to-all | bytes 278528 | tf_op jit(solution)/shard_map/all_to_all | solution.py:265
  59.3 0.0 copy-start
  59.3 0.0 copy-start.1
  59.3 0.2 turn.1
  59.5 24.7 %all_to_all.21.in_ref = bf16[32,33,2,128]{3,2,1,0:T(2,128)(2,1)S(1)} all-to-all(bf16[32,33,2,128]{3,2,1,0:T(2,128)(2,1)S(1)} %turn.1), channel_id=1, replica_groups=mesh['groups'=2,'zh'=4,'zl'=4,'x'=8,'tensor'=2] {'zl','x'}, dimensions={0} | all-to-all | bytes 1081344 | tf_op jit(solution)/shard_map/all_to_all | solution.py:276
  84.2 0.0 copy-done
  84.2 0.0 copy-done.1
  84.2 0.0 copy-start.3
  84.2 0.0 copy-start.4
  84.2 0.0 copy-start.5
  84.2 0.0 copy-start.6
  84.2 2.5 %attend.1 = bf16[16,33,2,128]{3,2,1,0:T(2,128)(2,1)S(1)} custom-call(f32[8,128]{1,0:T(8,128)S(1)} %get-tuple-element.7.facts_ref, bf16[32,33,2,128]{3,2,1,0:T(2,128)(2,1)S(1)} %all_to_all.21.in_ref, bf16[1,2048,512]{2,1,0:T(8,128)(2,1)S(1)} %copy-done, bf16[1,2048,512]{2,1,0:T(8,128)(2,1)S(1)} %copy-done.1), custom_call_target="tpu_custom_call" | custom-call | tf_op jit(solution)/shard_map/attend/pallas_call | solution.py:277
  86.7 22.0 %all_to_all.22.in_ref = bf16[16,33,2,128]{3,2,1,0:T(2,128)(2,1)S(1)} all-to-all(bf16[16,33,2,128]{3,2,1,0:T(2,128)(2,1)S(1)} %attend.1), channel_id=1, replica_groups=mesh['groups'=2,'zh'=4,'zl'=4,'x'=8,'tensor'=2] {'zh','zl'}, dimensions={0} | all-to-all | bytes 540672 | tf_op jit(solution)/shard_map/all_to_all | solution.py:291
  108.8 0.4 back.1
  109.2 20.3 %all_to_all.23.in_ref = bf16[32,17,2,128]{3,2,1,0:T(2,128)(2,1)S(1)} all-to-all(bf16[32,17,2,128]{3,2,1,0:T(2,128)(2,1)S(1)} %back.1), channel_id=1, replica_groups=mesh['groups'=2,'zh'=4,'zl'=4,'x'=8,'tensor'=2] {'zl','x'}, dimensions={0} | all-to-all | bytes 557056 | tf_op jit(solution)/shard_map/all_to_all | solution.py:300
  129.6 0.0 copy-done.3
  129.6 0.0 copy-done.4
  129.6 0.0 copy-done.5
  129.6 0.0 copy-done.6
  129.6 1.0 merge.1
  130.6 5.9 %psum.7 = f32[4,128]{1,0:T(4,128)S(1)} all-reduce(f32[4,128]{1,0:T(4,128)S(1)} %get-tuple-element.11), channel_id=1, replica_groups=mesh['groups'=2,'zh'=4,'zl'=4,'x'=8,'tensor'=2] {'tensor'}, use_global_device_ids=true, to_apply=%region_0.0 | all-reduce | flops 512 | bytes 4096 | tf_op jit(solution)/shard_map/psum | solution.py:314
  136.5 0.1 negate_reduce_fusion
  136.6 0.6 fusion
Async XLA Ops:
  2.6 0.8 copy-start.2
  59.3 25.0 %copy-start = (bf16[1,2048,512]{2,1,0:T(8,128)(2,1)S(1)}, bf16[1,2048,512]{2,1,0:T(8,128)(2,1)}, u32[]{:S(2)}) copy-start(bf16[1,2048,512]{2,1,0:T(8,128)(2,1)} %k_ref.1) | copy-start | bytes 6291460
  59.3 25.0 %copy-start.1 = (bf16[1,2048,512]{2,1,0:T(8,128)(2,1)S(1)}, bf16[1,2048,512]{2,1,0:T(8,128)(2,1)}, u32[]{:S(2)}) copy-start(bf16[1,2048,512]{2,1,0:T(8,128)(2,1)} %v_ref.1) | copy-start | bytes 6291460
  84.2 45.3 %copy-start.3 = (bf16[1,4,4096]{2,1,0:T(4,128)(2,1)S(1)}, bf16[1,4,4096]{2,1,0:T(4,128)(2,1)}, u32[]{:S(2)}) copy-start(bf16[1,4,4096]{2,1,0:T(4,128)(2,1)} %q_ref.3) | copy-start | bytes 98308
  84.2 45.3 %copy-start.4 = (bf16[4096]{0:T(1024)(128)(2,1)S(1)}, bf16[4096]{0:T(1024)(128)(2,1)}, u32[]{:S(2)}) copy-start(bf16[4096]{0:T(1024)(128)(2,1)} %rw_ref.1) | copy-start | bytes 24580
  84.2 45.3 %copy-start.5 = (bf16[1,4,512]{2,1,0:T(4,128)(2,1)S(1)}, bf16[1,4,512]{2,1,0:T(4,128)(2,1)}, u32[]{:S(2)}) copy-start(bf16[1,4,512]{2,1,0:T(4,128)(2,1)} %nk_ref.1) | copy-start | bytes 12292
  84.2 45.3 %copy-start.6 = (bf16[1,4,512]{2,1,0:T(4,128)(2,1)S(1)}, bf16[1,4,512]{2,1,0:T(4,128)(2,1)}, u32[]{:S(2)}) copy-start(bf16[1,4,512]{2,1,0:T(4,128)(2,1)} %nv_ref.1) | copy-start | bytes 12292

commit v6 on v4

--- a/solution.py
+++ b/solution.py
@@ -12,6 +12,7 @@
 CHILDREN = 2
 PAIR = 2
 TILE = 8
+HEAD_START = 6000
 GROUPS_DP = ("groups", "zh", "zl", "x")
 NEAR = ("zl", "x")
 FAR = ("zh", "zl")
@@ -42,6 +43,10 @@
     steps = q_ref.shape[1]
     pairs = out_ref.shape[1] - 1
     turns = steps // PAIR
+    @pl.when(lax.axis_index("tensor") == 1)
+    def _():
+        pl.delay(HEAD_START)
+
     facts = [parents_ref[0].astype(F32), lengths_ref[0].astype(F32), scores_ref[0]]
     for n, fact in enumerate(facts):
         facts_ref[n : n + 1, :] = jnp.full((1, HD), fact, F32)

time: 139 us -> 141 us (1.014)
  Pallas kernels: 4.57 us -> 10.5 us
  blocking collectives: 128 us -> 124 us
    pallas_call x1, Pallas kernels: 0.15 us -> 6.15 us  [per_device(): pl.pallas_call(functools.partial(send_kernel, columns), out_shape=(array(...]
    all_to_all x1, blocking collectives: 23.2 us -> 19.4 us  [per_device(): answers = lax.all_to_all(outputs, FAR, 0, 0, tiled=True)]
    all_to_all x1, blocking collectives: 48.8 us -> 51.6 us  [per_device(): asked = lax.all_to_all(turned, FAR, 0, 0, tiled=True)]
    all_to_all x1, blocking collectives: 21 us -> 19 us  [per_device(): pieces = lax.all_to_all(back, NEAR, 0, 0, tiled=True)]
where the time goes in v6:
time: 141 us; the launch traced here: 140 us
  blocking collectives  124 us (88%)
  Pallas kernels  10.5 us (7%)
  between operations  4.46 us (3%)
    all_to_all x1, blocking collectives, per_device(): asked = lax.all_to_all(turned, FAR, 0, 0, tiled=True)  51.6 us
    all_to_all x1, blocking collectives, per_device(): pieces = lax.all_to_all(sent, NEAR, 0, 0, tiled=True)  29 us
    all_to_all x1, blocking collectives, per_device(): answers = lax.all_to_all(outputs, FAR, 0, 0, tiled=True)  19.4 us
    all_to_all x1, blocking collectives, per_device(): pieces = lax.all_to_all(back, NEAR, 0, 0, tiled=True)  19 us
    pallas_call x1, Pallas kernels, per_device(): pl.pallas_call(functools.partial(send_kernel, columns), out_shape=(array(...  6.15 us
    psum x1, blocking collectives, per_device(): reward = lax.psum(partial_reward, 'tensor')[:, 0]  4.87 us

profile of v6, /device:TPU:65, one launch (start us, length us, event | category | flops | bytes accessed | tf_op | source)
XLA Modules:
  0.0 140.4 jit_solution(6107391633168427819)
XLA Ops:
  2.6 0.0 copy-start.2
  2.6 0.7 copy-done.2
  3.3 6.1 %send.1 = (bf16[32,17,2,128]{3,2,1,0:T(2,128)(2,1)S(1)}, f32[8,128]{1,0:T(8,128)S(1)}) custom-call(s32[1]{0:T(128)S(6)} %copy.13.parents_ref, s32[1]{0:T(128)S(6)} %copy.11.lengths_ref, f32[1]{0:T(128)S(6)} %copy.12.scores_ref, bf16[1,4,4096]{2,1,0:T(4,128)(2,1)S(1)} %copy-done.2), custom_call_target="tpu_custom_call" | custom-call | flops 10000000000 | bytes 67108864 | tf_op jit(solution)/shard_map/send/pallas_call | solution.py:262
  9.5 29.0 %all_to_all.20.in_ref = bf16[32,17,2,128]{3,2,1,0:T(2,128)(2,1)S(1)} all-to-all(bf16[32,17,2,128]{3,2,1,0:T(2,128)(2,1)S(1)} %get-tuple-element.8), channel_id=1, replica_groups=mesh['groups'=2,'zh'=4,'zl'=4,'x'=8,'tensor'=2] {'zl','x'}, dimensions={0} | all-to-all | bytes 557056 | tf_op jit(solution)/shard_map/all_to_all | solution.py:271
  38.5 0.0 copy-start
  38.5 0.0 copy-start.1
  38.5 0.5 turn.1
  39.0 51.6 %all_to_all.21.in_ref = bf16[16,33,2,128]{3,2,1,0:T(2,128)(2,1)S(1)} all-to-all(bf16[16,33,2,128]{3,2,1,0:T(2,128)(2,1)S(1)} %turn.1), channel_id=1, replica_groups=mesh['groups'=2,'zh'=4,'zl'=4,'x'=8,'tensor'=2] {'zh','zl'}, dimensions={0} | all-to-all | bytes 540672 | tf_op jit(solution)/shard_map/all_to_all | solution.py:282
  90.6 0.0 copy-done
  90.6 0.0 copy-done.1
  90.6 0.0 copy-start.3
  90.6 0.0 copy-start.4
  90.6 0.0 copy-start.5
  90.6 0.0 copy-start.6
  90.6 2.4 %attend.1 = bf16[16,33,2,128]{3,2,1,0:T(2,128)(2,1)S(1)} custom-call(f32[8,128]{1,0:T(8,128)S(1)} %get-tuple-element.7.facts_ref, bf16[16,33,2,128]{3,2,1,0:T(2,128)(2,1)S(1)} %all_to_all.21.in_ref, bf16[1,2048,512]{2,1,0:T(8,128)(2,1)S(1)} %copy-done, bf16[1,2048,512]{2,1,0:T(8,128)(2,1)S(1)} %copy-done.1), custom_call_target="tpu_custom_call" | custom-call | tf_op jit(solution)/shard_map/attend/pallas_call | solution.py:283
  93.0 19.4 %all_to_all.22.in_ref = bf16[16,33,2,128]{3,2,1,0:T(2,128)(2,1)S(1)} all-to-all(bf16[16,33,2,128]{3,2,1,0:T(2,128)(2,1)S(1)} %attend.1), channel_id=1, replica_groups=mesh['groups'=2,'zh'=4,'zl'=4,'x'=8,'tensor'=2] {'zh','zl'}, dimensions={0} | all-to-all | bytes 540672 | tf_op jit(solution)/shard_map/all_to_all | solution.py:297
  112.4 0.4 back.1
  112.9 19.0 %all_to_all.23.in_ref = bf16[32,17,2,128]{3,2,1,0:T(2,128)(2,1)S(1)} all-to-all(bf16[32,17,2,128]{3,2,1,0:T(2,128)(2,1)S(1)} %back.1), channel_id=1, replica_groups=mesh['groups'=2,'zh'=4,'zl'=4,'x'=8,'tensor'=2] {'zl','x'}, dimensions={0} | all-to-all | bytes 557056 | tf_op jit(solution)/shard_map/all_to_all | solution.py:306
  131.9 0.0 copy-done.3
  131.9 0.0 copy-done.4
  131.9 0.0 copy-done.5
  131.9 0.0 copy-done.6
  131.9 1.0 merge.1
  132.9 4.9 %psum.7 = f32[4,128]{1,0:T(4,128)S(1)} all-reduce(f32[4,128]{1,0:T(4,128)S(1)} %get-tuple-element.11), channel_id=1, replica_groups=mesh['groups'=2,'zh'=4,'zl'=4,'x'=8,'tensor'=2] {'tensor'}, use_global_device_ids=true, to_apply=%region_0.0 | all-reduce | flops 512 | bytes 4096 | tf_op jit(solution)/shard_map/psum | solution.py:320
  137.8 0.1 negate_reduce_fusion
  137.9 0.6 fusion
Async XLA Ops:
  2.6 0.8 copy-start.2
  38.5 52.1 %copy-start = (bf16[1,2048,512]{2,1,0:T(8,128)(2,1)S(1)}, bf16[1,2048,512]{2,1,0:T(8,128)(2,1)}, u32[]{:S(2)}) copy-start(bf16[1,2048,512]{2,1,0:T(8,128)(2,1)} %k_ref.1) | copy-start | bytes 6291460
  38.5 52.1 %copy-start.1 = (bf16[1,2048,512]{2,1,0:T(8,128)(2,1)S(1)}, bf16[1,2048,512]{2,1,0:T(8,128)(2,1)}, u32[]{:S(2)}) copy-start(bf16[1,2048,512]{2,1,0:T(8,128)(2,1)} %v_ref.1) | copy-start | bytes 6291460
  90.6 41.3 %copy-start.3 = (bf16[1,4,4096]{2,1,0:T(4,128)(2,1)S(1)}, bf16[1,4,4096]{2,1,0:T(4,128)(2,1)}, u32[]{:S(2)}) copy-start(bf16[1,4,4096]{2,1,0:T(4,128)(2,1)} %q_ref.3) | copy-start | bytes 98308
  90.6 41.3 %copy-start.4 = (bf16[4096]{0:T(1024)(128)(2,1)S(1)}, bf16[4096]{0:T(1024)(128)(2,1)}, u32[]{:S(2)}) copy-start(bf16[4096]{0:T(1024)(128)(2,1)} %rw_ref.1) | copy-start | bytes 24580
  90.6 41.3 %copy-start.5 = (bf16[1,4,512]{2,1,0:T(4,128)(2,1)S(1)}, bf16[1,4,512]{2,1,0:T(4,128)(2,1)}, u32[]{:S(2)}) copy-start(bf16[1,4,512]{2,1,0:T(4,128)(2,1)} %nk_ref.1) | copy-start | bytes 12292
  90.6 41.3 %copy-start.6 = (bf16[1,4,512]{2,1,0:T(4,128)(2,1)S(1)}, bf16[1,4,512]{2,1,0:T(4,128)(2,1)}, u32[]{:S(2)}) copy-start(bf16[1,4,512]{2,1,0:T(4,128)(2,1)} %nv_ref.1) | copy-start | bytes 12292

commit v7 on v5

--- a/solution.py
+++ b/solution.py
@@ -141,27 +141,29 @@
                 line = jnp.where(part == 3 * rows + n, extra, line)
             tails.append(line)
         item[j, CHILDREN * pairs] = jnp.concatenate(tails, axis=0).astype(BF16)
-    for b in range(out_ref.shape[0] // kv_heads):
-        out_ref[b * kv_heads : (b + 1) * kv_heads] = item[...]
+    for j in range(kv_heads):
+        for d in range(columns):
+            out_ref[j * columns + d] = item[j]
 
 
 def back_kernel(columns, in_ref, out_ref):
     pairs = out_ref.shape[1] - 1
     rows = pairs * PAIR
-    first = lax.axis_index("zh") * out_ref.shape[0]
+    mine = lax.axis_index("x")
     children = []
     for i in range(in_ref.shape[0]):
         tail = in_ref[i, CHILDREN * pairs].astype(F32)
         children.append([whole_number(tail[c : c + 1], 3 * rows) for c in range(CHILDREN)])
     for i in range(in_ref.shape[0]):
         for c in range(CHILDREN):
-            place = children[i][c] - first
-
-            @pl.when((place >= 0) & (place < out_ref.shape[0]))
+            child = children[i][c]
+
+            @pl.when((child >= 0) & (child % columns == mine))
             def _():
-                out_ref[place, :pairs] = in_ref[i, c * pairs : (c + 1) * pairs]
+                row = child // columns
+                out_ref[row, :pairs] = in_ref[i, c * pairs : (c + 1) * pairs]
                 tail = in_ref[i, CHILDREN * pairs].astype(F32)[c : c + 1]
-                out_ref[place, pairs] = jnp.broadcast_to(tail, (PAIR, HD)).astype(BF16)
+                out_ref[row, pairs] = jnp.broadcast_to(tail, (PAIR, HD)).astype(BF16)
 
 
 def merge_kernel(
@@ -172,15 +174,15 @@
     steps, heads = q_ref.shape[1], q_ref.shape[2] // HD
     kv_heads = nk_ref.shape[2] // HD
     size = steps * heads
-    column = whole_number(facts_ref[0:1, :], 0) % columns
+    first = whole_number(facts_ref[0:1, :], 0) // (columns * kv_heads) * kv_heads
     lane = lax.broadcasted_iota(jnp.int32, (rows, HD), 1)
     own = lane % rows == lax.broadcasted_iota(jnp.int32, (rows, HD), 0)
     own = own & (lane < 3 * rows)
     tops = []
     for j in range(kv_heads):
         for g in range(pairs):
-            came[j * rows + g * PAIR : j * rows + (g + 1) * PAIR, :] = in_ref[j * columns + column, g].astype(F32)
-        tail = in_ref[j * columns + column, pairs].astype(F32)[0:1]
+            came[j * rows + g * PAIR : j * rows + (g + 1) * PAIR, :] = in_ref[first + j, g].astype(F32)
+        tail = in_ref[first + j, pairs].astype(F32)[0:1]
         tops.append(jnp.sum(jnp.where(own, tail, 0.0), axis=-1, keepdims=True))
         if j == 0:
             base = 3 * rows + 1
@@ -276,7 +278,7 @@
     asked = lax.all_to_all(turned, NEAR, 0, 0, tiled=True)
     outputs = pl.pallas_call(
         attend_kernel,
-        out_shape=array(far, *both),
+        out_shape=array(near, *both),
         in_specs=[VMEM, VMEM, VMEM, VMEM],
         out_specs=VMEM,
         scratch_shapes=[
@@ -288,16 +290,16 @@
         compiler_params=limit(16),
         name="attend",
     )(facts, asked, cache_keys, cache_values)
-    answers = lax.all_to_all(outputs, FAR, 0, 0, tiled=True)
+    answers = lax.all_to_all(outputs, NEAR, 0, 0, tiled=True)
     back = pl.pallas_call(
         functools.partial(back_kernel, columns),
-        out_shape=array(near, *one),
+        out_shape=array(far, *one),
         in_specs=[VMEM],
         out_specs=VMEM,
         compiler_params=limit(4),
         name="back",
     )(answers)
-    pieces = lax.all_to_all(back, NEAR, 0, 0, tiled=True)
+    pieces = lax.all_to_all(back, FAR, 0, 0, tiled=True)
     output, partial_reward, inherited = pl.pallas_call(
         functools.partial(merge_kernel, columns),
         out_shape=(

time: 139 us -> 141 us (1.014)
  no operation moved by 1% of the time
where the time goes in v7:
time: 141 us
  blocking collectives  130 us (92%)
  Pallas kernels  4.99 us (4%)
  between operations  4.45 us (3%)
    all_to_all x1, blocking collectives, per_device(): pieces = lax.all_to_all(sent, FAR, 0, 0, tiled=True)  55.8 us
    all_to_all x1, blocking collectives, per_device(): asked = lax.all_to_all(turned, NEAR, 0, 0, tiled=True)  24.7 us
    all_to_all x1, blocking collectives, per_device(): answers = lax.all_to_all(outputs, NEAR, 0, 0, tiled=True)  24 us
    all_to_all x1, blocking collectives, per_device(): pieces = lax.all_to_all(back, FAR, 0, 0, tiled=True)  19.1 us
    psum x1, blocking collectives, per_device(): reward = lax.psum(partial_reward, 'tensor')[:, 0]  6.03 us

profile of v7, /device:TPU:65, one launch (start us, length us, event | category | flops | bytes accessed | tf_op | source)
XLA Modules:
  0.0 140.6 jit_solution(1197151009650537334)
XLA Ops:
  2.6 0.0 copy-start.2
  2.6 0.7 copy-done.2
  3.3 0.1 send.1
  3.4 55.8 %all_to_all.20.in_ref = bf16[16,17,2,128]{3,2,1,0:T(2,128)(2,1)S(1)} all-to-all(bf16[16,17,2,128]{3,2,1,0:T(2,128)(2,1)S(1)} %get-tuple-element.8), channel_id=1, replica_groups=mesh['groups'=2,'zh'=4,'zl'=4,'x'=8,'tensor'=2] {'zh','zl'}, dimensions={0} | all-to-all | bytes 278528 | tf_op jit(solution)/shard_map/all_to_all | solution.py:267
  59.3 0.0 copy-start
  59.3 0.0 copy-start.1
  59.3 0.2 turn.1
  59.5 24.7 %all_to_all.21.in_ref = bf16[32,33,2,128]{3,2,1,0:T(2,128)(2,1)S(1)} all-to-all(bf16[32,33,2,128]{3,2,1,0:T(2,128)(2,1)S(1)} %turn.1), channel_id=1, replica_groups=mesh['groups'=2,'zh'=4,'zl'=4,'x'=8,'tensor'=2] {'zl','x'}, dimensions={0} | all-to-all | bytes 1081344 | tf_op jit(solution)/shard_map/all_to_all | solution.py:278
  84.2 0.0 copy-done
  84.2 0.0 copy-done.1
  84.2 0.0 copy-start.3
  84.2 0.0 copy-start.4
  84.2 0.0 copy-start.5
  84.2 0.0 copy-start.6
  84.2 2.6 %attend.1 = bf16[32,33,2,128]{3,2,1,0:T(2,128)(2,1)S(1)} custom-call(f32[8,128]{1,0:T(8,128)S(1)} %get-tuple-element.7.facts_ref, bf16[32,33,2,128]{3,2,1,0:T(2,128)(2,1)S(1)} %all_to_all.21.in_ref, bf16[1,2048,512]{2,1,0:T(8,128)(2,1)S(1)} %copy-done, bf16[1,2048,512]{2,1,0:T(8,128)(2,1)S(1)} %copy-done.1), custom_call_target="tpu_custom_call" | custom-call | tf_op jit(solution)/shard_map/attend/pallas_call | solution.py:279
  86.9 24.0 %all_to_all.22.in_ref = bf16[32,33,2,128]{3,2,1,0:T(2,128)(2,1)S(1)} all-to-all(bf16[32,33,2,128]{3,2,1,0:T(2,128)(2,1)S(1)} %attend.1), channel_id=1, replica_groups=mesh['groups'=2,'zh'=4,'zl'=4,'x'=8,'tensor'=2] {'zl','x'}, dimensions={0} | all-to-all | bytes 1081344 | tf_op jit(solution)/shard_map/all_to_all | solution.py:293
  110.9 1.0 back.1
  111.9 19.1 %all_to_all.23.in_ref = bf16[16,17,2,128]{3,2,1,0:T(2,128)(2,1)S(1)} all-to-all(bf16[16,17,2,128]{3,2,1,0:T(2,128)(2,1)S(1)} %back.1), channel_id=1, replica_groups=mesh['groups'=2,'zh'=4,'zl'=4,'x'=8,'tensor'=2] {'zh','zl'}, dimensions={0} | all-to-all | bytes 278528 | tf_op jit(solution)/shard_map/all_to_all | solution.py:302
  131.0 0.0 copy-done.3
  131.0 0.0 copy-done.4
  131.0 0.0 copy-done.5
  131.0 0.0 copy-done.6
  131.0 1.0 merge.1
  132.1 6.0 %psum.7 = f32[4,128]{1,0:T(4,128)S(1)} all-reduce(f32[4,128]{1,0:T(4,128)S(1)} %get-tuple-element.11), channel_id=1, replica_groups=mesh['groups'=2,'zh'=4,'zl'=4,'x'=8,'tensor'=2] {'tensor'}, use_global_device_ids=true, to_apply=%region_0.0 | all-reduce | flops 512 | bytes 4096 | tf_op jit(solution)/shard_map/psum | solution.py:316
  138.1 0.1 negate_reduce_fusion
  138.2 0.6 fusion
Async XLA Ops:
  2.6 0.8 copy-start.2
  59.3 25.0 %copy-start = (bf16[1,2048,512]{2,1,0:T(8,128)(2,1)S(1)}, bf16[1,2048,512]{2,1,0:T(8,128)(2,1)}, u32[]{:S(2)}) copy-start(bf16[1,2048,512]{2,1,0:T(8,128)(2,1)} %k_ref.1) | copy-start | bytes 6291460
  59.3 25.0 %copy-start.1 = (bf16[1,2048,512]{2,1,0:T(8,128)(2,1)S(1)}, bf16[1,2048,512]{2,1,0:T(8,128)(2,1)}, u32[]{:S(2)}) copy-start(bf16[1,2048,512]{2,1,0:T(8,128)(2,1)} %v_ref.1) | copy-start | bytes 6291460
  84.2 46.8 %copy-start.3 = (bf16[1,4,4096]{2,1,0:T(4,128)(2,1)S(1)}, bf16[1,4,4096]{2,1,0:T(4,128)(2,1)}, u32[]{:S(2)}) copy-start(bf16[1,4,4096]{2,1,0:T(4,128)(2,1)} %q_ref.3) | copy-start | bytes 98308
  84.2 46.8 %copy-start.4 = (bf16[4096]{0:T(1024)(128)(2,1)S(1)}, bf16[4096]{0:T(1024)(128)(2,1)}, u32[]{:S(2)}) copy-start(bf16[4096]{0:T(1024)(128)(2,1)} %rw_ref.1) | copy-start | bytes 24580
  84.2 46.8 %copy-start.5 = (bf16[1,4,512]{2,1,0:T(4,128)(2,1)S(1)}, bf16[1,4,512]{2,1,0:T(4,128)(2,1)}, u32[]{:S(2)}) copy-start(bf16[1,4,512]{2,1,0:T(4,128)(2,1)} %nk_ref.1) | copy-start | bytes 12292
  84.2 46.8 %copy-start.6 = (bf16[1,4,512]{2,1,0:T(4,128)(2,1)S(1)}, bf16[1,4,512]{2,1,0:T(4,128)(2,1)}, u32[]{:S(2)}) copy-start(bf16[1,4,512]{2,1,0:T(4,128)(2,1)} %nv_ref.1) | copy-start | bytes 12292

commit v8 on v4

--- a/solution.py
+++ b/solution.py
@@ -19,7 +19,7 @@
 SMEM = pl.BlockSpec(memory_space=pltpu.SMEM)
 BF16 = jnp.bfloat16
 F32 = jnp.float32
-SLOW = pl.CostEstimate(flops=10**10, bytes_accessed=2**26, transcendentals=0)
+SLOW = pl.CostEstimate(flops=10**11, bytes_accessed=2**28, transcendentals=0)
 
 
 def limit(mib):
@@ -38,14 +38,17 @@
     return [part.astype(F32) for part in (first, second, third)]
 
 
-def send_kernel(columns, parents_ref, lengths_ref, scores_ref, q_ref, out_ref, facts_ref):
+def facts_kernel(parents_ref, lengths_ref, scores_ref, facts_ref):
+    facts = [parents_ref[0].astype(F32), lengths_ref[0].astype(F32), scores_ref[0]]
+    for n, fact in enumerate(facts):
+        facts_ref[n : n + 1, :] = jnp.full((1, HD), fact, F32)
+
+
+def send_kernel(columns, parents_ref, q_ref, out_ref):
     steps = q_ref.shape[1]
     pairs = out_ref.shape[1] - 1
     turns = steps // PAIR
-    facts = [parents_ref[0].astype(F32), lengths_ref[0].astype(F32), scores_ref[0]]
-    for n, fact in enumerate(facts):
-        facts_ref[n : n + 1, :] = jnp.full((1, HD), fact, F32)
-    parent = jnp.full((PAIR, HD), facts[0], F32).astype(BF16)
+    parent = jnp.full((PAIR, HD), parents_ref[0].astype(F32), F32).astype(BF16)
     for j in range(out_ref.shape[0] // columns):
         for g in range(pairs):
             h, t = j * (pairs // turns) + g // turns, g % turns * PAIR
@@ -254,15 +257,24 @@
     def array(*shape, kind=BF16):
         return jax.ShapeDtypeStruct(shape, kind)
 
-    sent, facts = pl.pallas_call(
+    sent = pl.pallas_call(
         functools.partial(send_kernel, columns),
-        out_shape=(array(near, *one), array(TILE, HD, kind=F32)),
-        in_specs=[SMEM, SMEM, SMEM, VMEM],
-        out_specs=(VMEM, VMEM),
+        out_shape=array(near, *one),
+        in_specs=[SMEM, VMEM],
+        out_specs=VMEM,
         compiler_params=limit(4),
         cost_estimate=SLOW,
         name="send",
-    )(parents, lengths, parent_scores, queries)
+    )(parents, queries)
+    facts = pl.pallas_call(
+        facts_kernel,
+        out_shape=array(TILE, HD, kind=F32),
+        in_specs=[SMEM, SMEM, SMEM],
+        out_specs=VMEM,
+        compiler_params=limit(4),
+        cost_estimate=SLOW,
+        name="facts",
+    )(parents, lengths, parent_scores)
     pieces = lax.all_to_all(sent, NEAR, 0, 0, tiled=True)
     turned = pl.pallas_call(
         functools.partial(turn_kernel, columns),

time: 139 us -> 141 us (1.014)
  blocking collectives: 128 us -> 50.2 us
  starting transfers between devices: 0 us -> 55.9 us
  waiting for transfers between devices: 0 us -> 20.9 us
  local copies, waits for them, and re-layouts: 0.78 us -> 2.37 us
    all_to_all x2 -> x0, blocking collectives: 77.8 us -> none  [the longest x1 48.8 us: per_device(): asked = lax.all_to_all(turned, FAR, 0, 0, tiled=True)]
    all_to_all x0 -> x2, starting transfers between devices: none -> 55.9 us  [the longest x1 36.4 us: per_device(): asked = lax.all_to_all(turned, FAR, 0, 0, tiled=True)]
    all_to_all x0 -> x2, waiting for transfers between devices: none -> 20.9 us  [the longest x1 12.6 us: per_device(): asked = lax.all_to_all(turned, FAR, 0, 0, tiled=True)]
    unnamed x14, local copies, waits for them, and re-layouts: 0.78 us -> 2.37 us
  transfers between devices with their start and end apart: 0 -> 2, of which waited for: 0 -> 2; matrix products, arithmetic and copies ran while one was open for 0% -> 0% of each run, Pallas kernels for 0% -> 0%
where the time goes in v8:
time: 141 us; the launch traced here: 140 us
  starting transfers between devices  55.9 us (40%)
  blocking collectives  50.2 us (36%)
  waiting for transfers between devices  20.9 us (15%)
  Pallas kernels  5.89 us (4%)
  between operations  4.46 us (3%)
  local copies, waits for them, and re-layouts  2.37 us (2%)
    all_to_all x1, starting transfers between devices, per_device(): asked = lax.all_to_all(turned, FAR, 0, 0, tiled=True)  36.4 us
    all_to_all x1, blocking collectives, per_device(): answers = lax.all_to_all(outputs, FAR, 0, 0, tiled=True)  23.2 us
    all_to_all x1, blocking collectives, per_device(): pieces = lax.all_to_all(back, NEAR, 0, 0, tiled=True)  21.3 us
    all_to_all x1, starting transfers between devices, per_device(): pieces = lax.all_to_all(sent, NEAR, 0, 0, tiled=True)  19.5 us
    all_to_all x1, waiting for transfers between devices, per_device(): asked = lax.all_to_all(turned, FAR, 0, 0, tiled=True)  12.6 us
    all_to_all x1, waiting for transfers between devices, per_device(): pieces = lax.all_to_all(sent, NEAR, 0, 0, tiled=True)  8.36 us
    psum x1, blocking collectives, per_device(): reward = lax.psum(partial_reward, 'tensor')[:, 0]  5.69 us
  transfers between devices with their start and end apart: 2, of which 2 were waited for; matrix products, arithmetic and copies ran while one was open for 0% of the time, Pallas kernels for 0%

profile of v8, /device:TPU:65, one launch (start us, length us, event | category | flops | bytes accessed | tf_op | source)
XLA Modules:
  0.0 140.4 jit_solution(16206121554897784865)
XLA Ops:
  1.3 0.0 copy-start.2
  1.3 0.7 copy-done.2
  2.0 0.8 send.1
  2.9 19.5 %all-to-all-start = ((bf16[32,17,2,128]{3,2,1,0:T(2,128)(2,1)}), bf16[32,17,2,128]{3,2,1,0:T(2,128)(2,1)S(1)}, u32[]{:S(2)}, u32[]{:S(2)}) async-start(bf16[32,17,2,128]{3,2,1,0:T(2,128)(2,1)} %send.1), calls=%async_computation | async-start | bytes 557056 | tf_op jit(solution)/shard_map/all_to_all | solution.py:278
  23.7 8.4 %all-to-all-done.in_ref = bf16[32,17,2,128]{3,2,1,0:T(2,128)(2,1)S(1)} async-done(((bf16[32,17,2,128]{3,2,1,0:T(2,128)(2,1)}), bf16[32,17,2,128]{3,2,1,0:T(2,128)(2,1)S(1)}, u32[]{:S(2)}, u32[]{:S(2)}) %all-to-all-start) | async-done | bytes 278560 | tf_op jit(solution)/shard_map/all_to_all | solution.py:278
  32.1 1.2 turn.1
  33.2 36.4 %all-to-all-start.1 = ((bf16[16,33,2,128]{3,2,1,0:T(2,128)(2,1)}), bf16[16,33,2,128]{3,2,1,0:T(2,128)(2,1)S(1)}, u32[]{:S(2)}, u32[]{:S(2)}) async-start(bf16[16,33,2,128]{3,2,1,0:T(2,128)(2,1)} %turn.1), calls=%async_computation.1 | async-start | bytes 540672 | tf_op jit(solution)/shard_map/all_to_all | solution.py:289
  69.6 0.0 copy-start
  69.6 12.6 %all-to-all-done.1.in_ref = bf16[16,33,2,128]{3,2,1,0:T(2,128)(2,1)S(1)} async-done(((bf16[16,33,2,128]{3,2,1,0:T(2,128)(2,1)}), bf16[16,33,2,128]{3,2,1,0:T(2,128)(2,1)S(1)}, u32[]{:S(2)}, u32[]{:S(2)}) %all-to-all-start.1) | async-done | bytes 270368 | tf_op jit(solution)/shard_map/all_to_all | solution.py:289
  82.2 0.0 copy-done
  82.2 0.0 copy-start.1
  82.2 1.6 %copy-done.1 = bf16[1,2048,512]{2,1,0:T(8,128)(2,1)S(1)} copy-done((bf16[1,2048,512]{2,1,0:T(8,128)(2,1)S(1)}, bf16[1,2048,512]{2,1,0:T(8,128)(2,1)}, u32[]{:S(2)}) %copy-start.1) | copy-done | bytes 2097176
  83.8 0.0 copy-start.3
  83.8 0.0 copy-start.4
  83.8 0.0 copy-start.5
  83.8 0.0 copy-start.6
  83.8 2.4 %attend.1 = bf16[16,33,2,128]{3,2,1,0:T(2,128)(2,1)S(1)} custom-call(f32[8,128]{1,0:T(8,128)S(1)} %facts.1.facts_ref, bf16[16,33,2,128]{3,2,1,0:T(2,128)(2,1)S(1)} %all-to-all-done.1.in_ref, bf16[1,2048,512]{2,1,0:T(8,128)(2,1)S(1)} %copy-done, bf16[1,2048,512]{2,1,0:T(8,128)(2,1)S(1)} %copy-done.1), custom_call_target="tpu_custom_call" | custom-call | tf_op jit(solution)/shard_map/attend/pallas_call | solution.py:290
  86.2 23.2 %all_to_all.20.in_ref = bf16[16,33,2,128]{3,2,1,0:T(2,128)(2,1)S(1)} all-to-all(bf16[16,33,2,128]{3,2,1,0:T(2,128)(2,1)S(1)} %attend.1), channel_id=1, replica_groups=mesh['groups'=2,'zh'=4,'zl'=4,'x'=8,'tensor'=2] {'zh','zl'}, dimensions={0} | all-to-all | bytes 540672 | tf_op jit(solution)/shard_map/all_to_all | solution.py:304
  109.4 0.4 back.1
  109.8 21.3 %all_to_all.21.in_ref = bf16[32,17,2,128]{3,2,1,0:T(2,128)(2,1)S(1)} all-to-all(bf16[32,17,2,128]{3,2,1,0:T(2,128)(2,1)S(1)} %back.1), channel_id=1, replica_groups=mesh['groups'=2,'zh'=4,'zl'=4,'x'=8,'tensor'=2] {'zl','x'}, dimensions={0} | all-to-all | bytes 557056 | tf_op jit(solution)/shard_map/all_to_all | solution.py:313
  131.1 0.0 copy-done.3
  131.1 0.0 copy-done.4
  131.1 0.0 copy-done.5
  131.1 0.0 copy-done.6
  131.2 1.0 merge.1
  132.2 5.7 %psum.7 = f32[4,128]{1,0:T(4,128)S(1)} all-reduce(f32[4,128]{1,0:T(4,128)S(1)} %get-tuple-element.7), channel_id=1, replica_groups=mesh['groups'=2,'zh'=4,'zl'=4,'x'=8,'tensor'=2] {'tensor'}, use_global_device_ids=true, to_apply=%region_0.0 | all-reduce | flops 512 | bytes 4096 | tf_op jit(solution)/shard_map/psum | solution.py:327
  137.9 0.1 negate_reduce_fusion
  138.0 0.6 fusion
  (1 shorter events, 0.0 us)
Async XLA Ops:
  1.3 0.8 copy-start.2
  2.9 29.2 %all-to-all-start = ((bf16[32,17,2,128]{3,2,1,0:T(2,128)(2,1)}), bf16[32,17,2,128]{3,2,1,0:T(2,128)(2,1)S(1)}, u32[]{:S(2)}, u32[]{:S(2)}) async-start(bf16[32,17,2,128]{3,2,1,0:T(2,128)(2,1)} %send.1), calls=%async_computation | async-start | bytes 557056 | tf_op jit(solution)/shard_map/all_to_all | solution.py:278
  33.2 49.0 %all-to-all-start.1 = ((bf16[16,33,2,128]{3,2,1,0:T(2,128)(2,1)}), bf16[16,33,2,128]{3,2,1,0:T(2,128)(2,1)S(1)}, u32[]{:S(2)}, u32[]{:S(2)}) async-start(bf16[16,33,2,128]{3,2,1,0:T(2,128)(2,1)} %turn.1), calls=%async_computation.1 | async-start | bytes 540672 | tf_op jit(solution)/shard_map/all_to_all | solution.py:289
  69.6 12.6 %copy-start = (bf16[1,2048,512]{2,1,0:T(8,128)(2,1)S(1)}, bf16[1,2048,512]{2,1,0:T(8,128)(2,1)}, u32[]{:S(2)}) copy-start(bf16[1,2048,512]{2,1,0:T(8,128)(2,1)} %k_ref.1) | copy-start | bytes 6291460
  82.2 1.6 %copy-start.1 = (bf16[1,2048,512]{2,1,0:T(8,128)(2,1)S(1)}, bf16[1,2048,512]{2,1,0:T(8,128)(2,1)}, u32[]{:S(2)}) copy-start(bf16[1,2048,512]{2,1,0:T(8,128)(2,1)} %v_ref.1) | copy-start | bytes 6291460
  83.8 47.4 %copy-start.3 = (bf16[1,4,4096]{2,1,0:T(4,128)(2,1)S(1)}, bf16[1,4,4096]{2,1,0:T(4,128)(2,1)}, u32[]{:S(2)}) copy-start(bf16[1,4,4096]{2,1,0:T(4,128)(2,1)} %q_ref.3) | copy-start | bytes 98308
  83.8 47.4 %copy-start.4 = (bf16[4096]{0:T(1024)(128)(2,1)S(1)}, bf16[4096]{0:T(1024)(128)(2,1)}, u32[]{:S(2)}) copy-start(bf16[4096]{0:T(1024)(128)(2,1)} %rw_ref.1) | copy-start | bytes 24580
  83.8 47.4 %copy-start.5 = (bf16[1,4,512]{2,1,0:T(4,128)(2,1)S(1)}, bf16[1,4,512]{2,1,0:T(4,128)(2,1)}, u32[]{:S(2)}) copy-start(bf16[1,4,512]{2,1,0:T(4,128)(2,1)} %nk_ref.1) | copy-start | bytes 12292
  83.8 47.4 %copy-start.6 = (bf16[1,4,512]{2,1,0:T(4,128)(2,1)S(1)}, bf16[1,4,512]{2,1,0:T(4,128)(2,1)}, u32[]{:S(2)}) copy-start(bf16[1,4,512]{2,1,0:T(4,128)(2,1)} %nv_ref.1) | copy-start | bytes 12292
